TPU v7x, 8 devices: a whole 2x2x1 slice. The times are simulated.
8 devices in a mesh: dp: 2 (over z, y), tp: 4 (over x, core).
Axes of the slice: x: 2, y: 2, z: 1, core: 2. Of those that a mesh axis runs over, the one named last changes fastest.
Arguments:
- x_rows: bfloat16 [8192, 1536], P(('dp', 'tp')), parts along dimension 0
- norm_gain: float32 [1536], replicated
- w_q: bfloat16 [1536, 12, 128], P(None, 'tp')
- w_k: bfloat16 [1536, 256], P(None, 'tp')
- w_v: bfloat16 [1536, 256], P(None, 'tp')
Outputs:
- output 1: bfloat16 [8192, 12, 128], P('dp', 'tp'), parts along dimension 0
- output 2: bfloat16 [8192, 4, 128], P('dp', 'tp'), parts along dimension 0
- output 3: bfloat16 [8192, 4, 128], P('dp', 'tp'), parts along dimension 0
There are 2 independent parts. A program takes and returns all parts, laid end to end along the dimension named above; an argument that names none is the same for every part.
All inputs are finite; a program needn't handle non-finite values.
Results may differ from a plain program's by a relative error of at most 0.001.
Values are sent between devices in bfloat16 or wider.
A program may use at most 1 GiB of HBM per device.

v0:
```python
import jax
import jax.numpy as jnp
from jax import lax
from jax.sharding import PartitionSpec as P

EPSILON = 1e-6


def solution(mesh):
    group_size = mesh.shape["tp"]

    def head_pieces(piece, head_share):
        member = lax.axis_index("tp") % head_share
        received = [piece]
        for step_ahead in range(1, head_share):
            send_pairs = [(source, (source // head_share) * head_share + (source % head_share - step_ahead) % head_share) for source in range(group_size)]
            received.append(lax.ppermute(piece, "tp", send_pairs))
        joined = jnp.concatenate(received, axis=1)
        return jnp.roll(joined, member * piece.shape[1], axis=1)

    def local_step(x_rows, norm_gain, w_q, w_k, w_v):
        x_wide = x_rows.astype(jnp.float32)
        mean_sq = jnp.mean(x_wide * x_wide, axis=-1, keepdims=True)
        normed = (x_wide * lax.rsqrt(mean_sq + EPSILON) * norm_gain).astype(jnp.bfloat16)
        gathered = lax.all_gather(normed, "tp", axis=0, tiled=True)
        q_local = jnp.einsum("td,dhe->the", gathered, w_q, preferred_element_type=jnp.float32).astype(jnp.bfloat16)
        k_piece = jnp.dot(gathered, w_k, preferred_element_type=jnp.float32).astype(jnp.bfloat16)
        v_piece = jnp.dot(gathered, w_v, preferred_element_type=jnp.float32).astype(jnp.bfloat16)
        head_share = w_q.shape[2] // w_k.shape[1]
        k_head = head_pieces(k_piece, head_share)
        v_head = head_pieces(v_piece, head_share)
        return q_local, k_head[:, None, :], v_head[:, None, :]

    return jax.shard_map(local_step, mesh=mesh, in_specs=(P(("dp", "tp"), None), P(None), P(None, "tp", None), P(None, "tp"), P(None, "tp")), out_specs=(P("dp", "tp", None), P("dp", "tp", None), P("dp", "tp", None)), check_vma=False)
```

profile of v0, /device:TPU:1, one launch (start us, length us, event | category | flops | bytes accessed | tf_op | source)
XLA Modules:
  0.0 128.2 jit_solution(8683394718836104650)
XLA Ops:
  7.2 0.0 copy-start
  7.2 0.0 copy-start.5
  7.2 0.0 all-gather.2.cloned.1.call-start
  7.2 0.0 copy-start.2
  7.2 2.7 %fusion.2 = f32[1024]{0:T(1024)S(1)} fusion(bf16[1024,1536]{1,0:T(8,128)(2,1)} %param.7), kind=kLoop, calls=%fused_computation.4 | loop fusion | flops 4717568 | bytes 3149824 | tf_op jit(solution)/shard_map/reduce_sum | solution.py:23
  10.0 0.0 copy-done.5
  10.0 0.1 copy-done.2
  10.1 2.4 %fusion.4 = bf16[1024,1536]{1,0:T(8,128)(2,1)} fusion(bf16[1024,1536]{1,0:T(8,128)(2,1)S(1)} %copy-done.2, f32[1536]{0:T(1024)S(1)} %copy-done.5, f32[1024]{0:T(1024)S(1)} %add_rsqrt_fusion), kind=kLoop, calls=%fused_computation.6 | loop fusion | flops 6291456 | bytes 6301696 | tf_op jit(solution)/shard_map/convert_element_type | solution.py:24
  12.6 0.0 all-gather.2.cloned.1.call-update
  12.6 0.0 copy-start.4
  12.6 82.3 %all-gather.2.cloned.1.call-done = bf16[4096,1536]{1,0:T(8,128)(2,1)} async-done(((bf16[1024,1536]{1,0:T(8,128)(2,1)}), bf16[4096,1536]{1,0:T(8,128)(2,1)}) %all-gather.2.cloned.1.call-update) | async-done | bytes 12582928 | tf_op jit(solution)/shard_map/all_gather | solution.py:25
  94.9 0.0 copy-done.3
  94.9 8.6 %convolution_convert_fusion.1 = bf16[4096,64]{0,1:T(8,128)(2,1)S(1)} fusion(bf16[4096,1536]{1,0:T(8,128)(2,1)} %all-gather.2.cloned.1.call-done, bf16[1536,64]{0,1:T(8,128)(2,1)S(1)} %copy-done.3), kind=kOutput, calls=%fused_computation.9 | convolution fusion | flops 805568512 | bytes 13303808 | tf_op jit(solution)/shard_map/dot_general | solution.py:27
  103.5 0.3 collective-permute-start
  103.8 0.0 copy-done.1
  103.8 3.9 %convolution_convert_fusion = bf16[4096,64]{0,1:T(8,128)(2,1)S(1)} fusion(bf16[4096,1536]{1,0:T(8,128)(2,1)S(1)} %copy-done.1, bf16[1536,64]{0,1:T(8,128)(2,1)S(1)} %copy-done.4), kind=kOutput, calls=%fused_computation.8 | convolution fusion | flops 805568512 | bytes 13303808 | tf_op jit(solution)/shard_map/dot_general | solution.py:28
  107.7 0.3 collective-permute-start.1
  108.0 8.2 %fusion.5 = bf16[4096,3,128]{2,0,1:T(8,128)(2,1)} fusion(bf16[1536,3,128]{2,0,1:T(8,128)(2,1)S(1)} %copy-done, bf16[4096,1536]{1,0:T(8,128)(2,1)S(1)} %copy-done.1), kind=kOutput, calls=%fused_computation.7 | convolution fusion | flops 4833411072 | bytes 16908288 | tf_op jit(solution)/shard_map/td,dhe->the/dot_general | solution.py:26
  116.2 0.0 collective-permute-done
  116.2 1.2 fusion.12
  117.5 1.3 %copy.8 = bf16[4096,128]{1,0:T(8,128)(2,1)} copy(bf16[4096,128]{0,1:T(8,128)(2,1)S(1)} %fusion.12) | data formatting | bytes 2097152 | tf_op jit(solution)/shard_map/jit(_roll_dynamic)/dynamic_slice | solution.py:19
  118.8 0.0 collective-permute-done.1
  118.8 1.2 fusion.9
  120.0 1.3 %copy.9 = bf16[4096,128]{1,0:T(8,128)(2,1)} copy(bf16[4096,128]{0,1:T(8,128)(2,1)S(1)} %fusion.9) | data formatting | bytes 2097152 | tf_op jit(solution)/shard_map/jit(_roll_dynamic)/dynamic_slice | solution.py:19
  (5 shorter events, 0.0 us)
Async XLA Ops:
  7.2 100.8 %copy-start = (bf16[1536,3,128]{2,0,1:T(8,128)(2,1)S(1)}, bf16[1536,3,128]{2,0,1:T(8,128)(2,1)}, u32[]{:S(2)}) copy-start(bf16[1536,3,128]{2,0,1:T(8,128)(2,1)} %param.9) | copy-start | bytes 3538948
  7.2 2.8 %copy-start.5 = (f32[1536]{0:T(1024)S(1)}, f32[1536]{0:T(1024)}, u32[]{:S(2)}) copy-start(f32[1536]{0:T(1024)} %param.8) | copy-start | bytes 18436
  7.2 87.7 %all-gather.2.cloned.1.call-start = ((), (), s32[]{:S(2)}) async-start(), calls=%async_computation | async-start | bytes 15728640 | tf_op jit(solution)/shard_map/all_gather | solution.py:25
  7.2 2.9 %copy-start.2 = (bf16[1024,1536]{1,0:T(8,128)(2,1)S(1)}, bf16[1024,1536]{1,0:T(8,128)(2,1)}, u32[]{:S(2)}) copy-start(bf16[1024,1536]{1,0:T(8,128)(2,1)} %param.7) | copy-start | bytes 9437188
  12.6 82.4 %copy-start.3 = (bf16[1536,64]{0,1:T(8,128)(2,1)S(1)}, bf16[1536,64]{0,1:T(8,128)(2,1)}, u32[]{:S(2)}) copy-start(bf16[1536,64]{0,1:T(8,128)(2,1)} %param.10) | copy-start | bytes 589828
  12.6 91.2 %copy-start.4 = (bf16[1536,64]{0,1:T(8,128)(2,1)S(1)}, bf16[1536,64]{0,1:T(8,128)(2,1)}, u32[]{:S(2)}) copy-start(bf16[1536,64]{0,1:T(8,128)(2,1)} %param.11) | copy-start | bytes 589828
  94.9 8.9 %copy-start.1 = (bf16[4096,1536]{1,0:T(8,128)(2,1)S(1)}, bf16[4096,1536]{1,0:T(8,128)(2,1)}, u32[]{:S(2)}) copy-start(bf16[4096,1536]{1,0:T(8,128)(2,1)} %all-gather.2.cloned.1.call-done) | copy-start | bytes 37748740
  103.5 12.7 %collective-permute-start = (bf16[4096,64]{0,1:T(8,128)(2,1)S(1)}, bf16[4096,64]{0,1:T(8,128)(2,1)S(1)}, u32[]{:S(2)}, u32[]{:S(2)}) collective-permute-start(bf16[4096,64]{0,1:T(8,128)(2,1)S(1)} %convolution_convert_fusion.1), channel_id=1, source_target_pairs={{0,1},{1,0},{2,3},{3,2},{4,5},{5,4},{6,7},{7,6}} | collective-permute-start | bytes 1572872 | tf_op jit(solution)/shard_map/ppermute | solution.py:17
  107.7 11.1 %collective-permute-start.1 = (bf16[4096,64]{0,1:T(8,128)(2,1)S(1)}, bf16[4096,64]{0,1:T(8,128)(2,1)S(1)}, u32[]{:S(2)}, u32[]{:S(2)}) collective-permute-start(bf16[4096,64]{0,1:T(8,128)(2,1)S(1)} %convolution_convert_fusion), channel_id=1, source_target_pairs={{0,1},{1,0},{2,3},{3,2},{4,5},{5,4},{6,7},{7,6}} | collective-permute-start | bytes 1572872 | tf_op jit(solution)/shard_map/ppermute | solution.py:17
Sparse Core Ops, SparseCore 0:
  12.7 82.1 all-gather.1
where the time goes:
time: 129 us; the launch traced here: 128 us
  waiting for transfers between devices  82.3 us (64%)
  matrix products  20.7 us (16%)
  between operations  14.1 us (11%)
  other arithmetic  7.63 us (6%)
  local copies, waits for them, and re-layouts  2.79 us (2%)
    all_gather x1, waiting for transfers between devices, local_step(): gathered = lax.all_gather(normed, 'tp', axis=0, tiled=True)  82.3 us
    dot_general x1, matrix products, local_step(): jnp.dot(gathered, w_k, preferred_element_type=jnp.float32)  8.59 us
    dot_general x1, matrix products, local_step(): jnp.einsum('td,dhe->the', gathered, w_q, preferred_element_type=jnp.float32)  8.23 us
    dot_general x1, matrix products, local_step(): jnp.dot(gathered, w_v, preferred_element_type=jnp.float32)  3.88 us
    reduce_sum x1, other arithmetic, local_step(): mean_sq = jnp.mean(x_wide * x_wide, axis=-1, keepdims=True)  2.72 us
    dynamic_slice x2, local copies, waits for them, and re-layouts, head_pieces(): return jnp.roll(joined, member * piece.shape[1], axis=1)  2.62 us
  transfers between devices with their start and end apart: 3, of which 1 were waited for; matrix products, arithmetic and copies ran while one was open for 11% of the time, Pallas kernels for 0%

commit v1 on v0

v1 whole, which is shorter than its diff:
```python
import functools

import jax
import jax.numpy as jnp
from jax import lax
from jax.experimental import pallas as pl
from jax.experimental.pallas import tpu as pltpu
from jax.sharding import PartitionSpec as P

EPSILON = 1e-6
MESH = pl.DeviceIdType.MESH
LANES = 128
K_PIECE, V_PIECE, FIRST_HEAD = 0, 1, 2


def qkv_kernel(
    x_hbm, gain_hbm, wq_hbm, wk_hbm, wv_hbm,
    q_out, k_out, v_out,
    rows_buf, gain_buf, wq_buf, wkv_buf, q_stage, kv_stage,
    x_sem, gain_sem, load_sem,
    part_send, part_recv, link_send, link_recv, core_send, core_recv, side_send, side_recv, last_send, last_recv,
    near_send, near_recv, far_send, far_recv, cross_send, cross_recv, pass_send, pass_recv,
    *, norm_tile, dot_tile,
):
    n_rows, depth = rows_buf.shape
    heads = wq_hbm.shape[0]
    share = wk_hbm.shape[0]
    half = depth // 2
    pieces = FIRST_HEAD + heads

    group, member = lax.axis_index("dp"), lax.axis_index("tp")
    chip, core = member // 2, member % 2
    partner = (group, chip * 2 + (1 - core))
    across = (group, (1 - chip) * 2 + core)
    across_other = (group, (1 - chip) * 2 + (1 - core))
    beside = (1 - group, member)

    sources = [wk_hbm, wv_hbm] + [wq_hbm.at[h] for h in range(heads)]

    def piece_at(j, slot, depth_half=None):
        if j < FIRST_HEAD:
            rows = pl.ds(pl.multiple_of(j * 2 * share + core * share, share), share)
            if depth_half is None:
                return wkv_buf.at[slot // 2, rows]
            return wkv_buf.at[slot // 2, rows, pl.ds(pl.multiple_of(depth_half * half, half), half)]
        if depth_half is None:
            return wq_buf.at[slot, j - FIRST_HEAD]
        return wq_buf.at[slot, j - FIRST_HEAD, pl.ds(pl.multiple_of(depth_half * half, half), half)]

    loads = [pltpu.make_async_copy(sources[j], piece_at(j, 0), load_sem.at[j]) for j in range(pieces)]
    for load in loads:
        load.start()
    gain_load = pltpu.make_async_copy(gain_hbm, gain_buf, gain_sem)
    gain_load.start()
    n_tiles = n_rows // norm_tile
    x_loads = [
        pltpu.make_async_copy(x_hbm.at[pl.ds(i * norm_tile, norm_tile)], rows_buf.at[pl.ds(i * norm_tile, norm_tile)], x_sem.at[i])
        for i in range(n_tiles)
    ]
    for load in x_loads:
        load.start()

    barrier = pltpu.get_barrier_semaphore()
    for other in (across, beside, across_other, partner):
        pl.semaphore_signal(barrier, inc=1, device_id=other, device_id_type=MESH)
    pl.semaphore_wait(barrier, 4)

    def remote(src, dst, send, recv, device):
        return pltpu.make_async_remote_copy(src_ref=src, dst_ref=dst, send_sem=send, recv_sem=recv, device_id=device, device_id_type=MESH)

    part, link, hand, side, last = [], [], [], [], []
    for j in range(pieces):
        part.append(remote(piece_at(j, 0), piece_at(j, 0 if j < FIRST_HEAD else 1), part_send.at[j], part_recv.at[j], partner))
        link.append(remote(piece_at(j, 0, group), piece_at(j, 2, group), link_send.at[j], link_recv.at[j], across))
        arrived, other_half = piece_at(j, 2, group), piece_at(j, 2, 1 - group)
        hand.append(remote(arrived, piece_at(j, 2 if j < FIRST_HEAD else 3, group), core_send.at[j], core_recv.at[j], partner))
        side.append(remote(arrived, arrived, side_send.at[j], side_recv.at[j], beside))
        last.append(remote(other_half, piece_at(j, 2 if j < FIRST_HEAD else 3, 1 - group), last_send.at[j], last_recv.at[j], partner))

    my_rows = pl.ds(pl.multiple_of(member * n_rows, n_rows), n_rows)
    across_rows = pl.ds(pl.multiple_of(((1 - chip) * 2 + core) * n_rows, n_rows), n_rows)
    near = [remote(k_out.at[0, my_rows], k_out.at[0, my_rows], near_send.at[0], near_recv.at[0], partner),
            remote(v_out.at[0, my_rows], v_out.at[0, my_rows], near_send.at[1], near_recv.at[1], partner)]
    far = [remote(kv_stage.at[0], k_out.at[0, my_rows], far_send.at[0], far_recv.at[0], across),
           remote(kv_stage.at[1], v_out.at[0, my_rows], far_send.at[1], far_recv.at[1], across)]
    passed = [remote(k_out.at[0, across_rows], k_out.at[0, across_rows], pass_send.at[0], pass_recv.at[0], partner),
              remote(v_out.at[0, across_rows], v_out.at[0, across_rows], pass_send.at[1], pass_recv.at[1], partner)]
    cross = []
    for h in range(heads):
        near.append(remote(q_stage.at[0, h], q_out.at[h, my_rows], near_send.at[2 + h], near_recv.at[2 + h], partner))
        far.append(remote(q_stage.at[1, h], q_out.at[h, my_rows], far_send.at[2 + h], far_recv.at[2 + h], across))
        cross.append(remote(q_stage.at[2, h], q_out.at[h, my_rows], cross_send.at[h], cross_recv.at[h], across_other))

    for j in range(pieces):
        loads[j].wait()
        link[j].start()
        part[j].start()

    gain_load.wait()
    chunks = depth // LANES
    sub = 64

    for i in range(n_tiles):
        x_loads[i].wait()

    def norm_step(s, carry):
        here = pl.ds(pl.multiple_of(s * sub, sub), sub)
        total = jnp.zeros((sub, LANES), jnp.float32)
        for c in range(chunks):
            wide = rows_buf[here, c * LANES:(c + 1) * LANES].astype(jnp.float32)
            total = total + wide * wide
        scale = lax.rsqrt(jnp.sum(total, axis=-1, keepdims=True) / depth + EPSILON)
        for c in range(chunks):
            cols = slice(c * LANES, (c + 1) * LANES)
            wide = rows_buf[here, cols].astype(jnp.float32)
            rows_buf[here, cols] = (wide * scale * gain_buf[cols][None, :]).astype(jnp.bfloat16)
        return carry

    lax.fori_loop(0, n_rows // sub, norm_step, 0)

    def over_tiles(step):
        lax.fori_loop(0, n_rows // dot_tile, lambda i, carry: (step(i * dot_tile), carry)[1], 0)

    def q_block(slot, h, store):
        def step(start):
            tile = rows_buf[pl.ds(pl.multiple_of(start, dot_tile), dot_tile), :]
            store(start, jnp.dot(tile, wq_buf[slot, h], preferred_element_type=jnp.float32).astype(jnp.bfloat16))
        over_tiles(step)

    def kv_block(which, store):
        def step(start):
            tile = rows_buf[pl.ds(pl.multiple_of(start, dot_tile), dot_tile), :]
            both = lax.dot_general(tile, wkv_buf[which], (((1,), (1,)), ((), ())), preferred_element_type=jnp.float32)
            store(start, both.astype(jnp.bfloat16))
        over_tiles(step)

    def rows_at(start):
        return pl.ds(pl.multiple_of(start, dot_tile), dot_tile)

    def own_rows_at(start):
        return pl.ds(pl.multiple_of(member * n_rows + start, dot_tile), dot_tile)

    def own_q(h):
        def store(start, value):
            q_out[h, own_rows_at(start), :] = value
        q_block(0, h, store)

    def staged_q(stage, slot, h):
        def store(start, value):
            q_stage[stage, h, rows_at(start), :] = value
        q_block(slot, h, store)

    def own_kv():
        def store(start, value):
            k_out[0, own_rows_at(start), :] = value[:, :LANES]
            v_out[0, own_rows_at(start), :] = value[:, LANES:]
        kv_block(0, store)

    def far_kv():
        def store(start, value):
            kv_stage[0, rows_at(start), :] = value[:, :LANES]
            kv_stage[1, rows_at(start), :] = value[:, LANES:]
        kv_block(1, store)

    def from_link(j):
        link[j].wait_recv()
        side[j].start()
        hand[j].start()

    def from_side(j):
        side[j].wait_recv()
        last[j].start()

    def complete(j):
        hand[j].wait_recv()
        last[j].wait_recv()

    from_link(K_PIECE)
    from_link(V_PIECE)
    part[K_PIECE].wait_recv()
    part[V_PIECE].wait_recv()
    own_kv()
    from_side(K_PIECE)
    near[0].start()
    near[1].start()
    from_link(2)
    from_side(V_PIECE)
    own_q(0)
    complete(K_PIECE)
    complete(V_PIECE)
    far_kv()
    own_q(1)
    far[0].start()
    far[1].start()
    from_link(3)
    own_q(2)
    from_side(2)
    staged_q(1, 2, 0)
    from_link(4)
    complete(2)
    staged_q(2, 3, 0)
    far[2].start()
    from_side(3)
    staged_q(1, 2, 1)
    cross[0].start()
    complete(3)
    staged_q(2, 3, 1)
    far[3].start()
    from_side(4)
    staged_q(1, 2, 2)
    cross[1].start()
    complete(4)
    staged_q(2, 3, 2)
    far[4].start()
    for h in range(heads):
        part[FIRST_HEAD + h].wait_recv()
        staged_q(0, 1, h)
        if h == 0:
            cross[2].start()
        else:
            near[2 + h - 1].start()
    far[0].wait_recv()
    passed[0].start()
    far[1].wait_recv()
    passed[1].start()
    near[2 + heads - 1].start()

    for copy in part + link + hand + side + last:
        copy.wait_send()
    for copy in near:
        copy.wait()
    for copy in passed:
        copy.wait()
    for j, copy in enumerate(far):
        copy.wait_send()
        if j >= FIRST_HEAD:
            copy.wait_recv()
    for copy in cross:
        copy.wait()


def solution(mesh):
    def local_step(x_rows, norm_gain, w_q, w_k, w_v):
        n_rows, depth = x_rows.shape
        heads, width = w_q.shape[1:]
        share = w_k.shape[1]
        members = mesh.shape["tp"]
        pieces = FIRST_HEAD + heads
        all_rows = members * n_rows
        dma = pltpu.SemaphoreType.DMA
        norm_tile = n_rows // 4
        out_spec = pl.BlockSpec(memory_space=pltpu.VMEM)
        hbm = pl.BlockSpec(memory_space=pltpu.HBM)
        q, k, v = pl.pallas_call(
            functools.partial(qkv_kernel, norm_tile=norm_tile, dot_tile=256),
            out_shape=(
                jax.ShapeDtypeStruct((heads, all_rows, width), jnp.bfloat16),
                jax.ShapeDtypeStruct((1, all_rows, width), jnp.bfloat16),
                jax.ShapeDtypeStruct((1, all_rows, width), jnp.bfloat16),
            ),
            in_specs=[hbm] * 5,
            out_specs=(out_spec,) * 3,
            scratch_shapes=[
                pltpu.VMEM((n_rows, depth), jnp.bfloat16),
                pltpu.VMEM((depth,), jnp.float32),
                pltpu.VMEM((4, heads, depth, width), jnp.bfloat16),
                pltpu.VMEM((2, 4 * share, depth), jnp.bfloat16),
                pltpu.VMEM((3, heads, n_rows, width), jnp.bfloat16),
                pltpu.VMEM((2, n_rows, width), jnp.bfloat16),
                dma((4,)), dma(()), dma((pieces,)),
                *[dma((pieces,)) for _ in range(10)],
                dma((pieces,)), dma((pieces,)), dma((pieces,)), dma((pieces,)),
                dma((heads,)), dma((heads,)), dma((2,)), dma((2,)),
            ],
            compiler_params=pltpu.CompilerParams(collective_id=0, has_side_effects=True, vmem_limit_bytes=36 * 1024 * 1024),
            cost_estimate=pl.CostEstimate(flops=2 * n_rows * depth * 2048, bytes_accessed=16 * 1024 * 1024, transcendentals=0),
            name="qkv",
        )(*[pltpu.with_memory_space_constraint(a, pltpu.HBM) for a in (x_rows, norm_gain, w_q.transpose(1, 0, 2), w_k.T, w_v.T)])
        return q.transpose(1, 0, 2), k.transpose(1, 0, 2), v.transpose(1, 0, 2)

    return jax.shard_map(
        local_step, mesh=mesh,
        in_specs=(P(("dp", "tp"), None), P(None), P(None, "tp", None), P(None, "tp"), P(None, "tp")),
        out_specs=(P("dp", "tp", None), P("dp", "tp", None), P("dp", "tp", None)),
        check_vma=False,
    )
```

time: 129 us -> 71.2 us (0.55)
  waiting for transfers between devices: 82.3 us -> 0 us
  Pallas kernels: 0 us -> 66.9 us
  matrix products: 20.7 us -> 0 us
  between operations: 14.1 us -> 0.64 us
  other arithmetic: 7.63 us -> 0 us
    all_gather x1 -> x0, waiting for transfers between devices: 82.3 us -> none  [local_step(): gathered = lax.all_gather(normed, 'tp', axis=0, tiled=True)]
    pallas_call x0 -> x1, Pallas kernels: none -> 66.9 us  [local_step(): pl.pallas_call(functools.partial(qkv_kernel, norm_tile=norm_tile, dot_til...]
    dot_general x3 -> x0, matrix products: 20.7 us -> none  [the longest x1 8.59 us: local_step(): jnp.dot(gathered, w_k, preferred_element_type=jnp.float32)]
    unnamed x12 -> x3, local copies, waits for them, and re-layouts: 0.17 us -> 3.61 us
    reduce_sum x1 -> x0, other arithmetic: 2.72 us -> none  [local_step(): mean_sq = jnp.mean(x_wide * x_wide, axis=-1, keepdims=True)]
    dynamic_slice x2 -> x0, local copies, waits for them, and re-layouts: 2.62 us -> none  [head_pieces(): return jnp.roll(joined, member * piece.shape[1], axis=1)]
    concatenate x2 -> x0, other arithmetic: 2.46 us -> none  [head_pieces(): return jnp.roll(joined, member * piece.shape[1], axis=1)]
    convert_element_type x1 -> x0, other arithmetic: 2.45 us -> none  [local_step(): (x_wide * lax.rsqrt(mean_sq + EPSILON) * norm_gain).astype(jnp.bfloat16)]
  transfers between devices with their start and end apart: 3 -> 0, of which waited for: 1 -> 0; matrix products, arithmetic and copies ran while one was open for 11% -> 0% of each run, Pallas kernels for 0% -> 0%
where the time goes in v1:
time: 71.2 us; the launch traced here: 71.1 us
  Pallas kernels  66.9 us (94%)
  local copies, waits for them, and re-layouts  3.61 us (5%)
    pallas_call x1, Pallas kernels, local_step(): pl.pallas_call(functools.partial(qkv_kernel, norm_tile=norm_tile, dot_til...  66.9 us
    unnamed x3, local copies, waits for them, and re-layouts  3.61 us

profile of v1, /device:TPU:1, one launch (start us, length us, event | category | flops | bytes accessed | tf_op | source)
XLA Modules:
  0.0 71.1 jit_solution(7309721474133332135)
XLA Ops:
  0.6 66.9 %qkv.1 = (bf16[3,4096,128]{2,1,0:T(8,128)(2,1)S(1)}, bf16[1,4096,128]{2,1,0:T(8,128)(2,1)S(1)}, bf16[1,4096,128]{2,1,0:T(8,128)(2,1)S(1)}) custom-call(bf16[1024,1536]{1,0:T(8,128)(2,1)} %x_hbm.1, f32[1536]{0:T(1024)} %gain_hbm.1, bf16[3,1536,128]{2,1,0:T(8,128)(2,1)} %bitcast.9, bf16[64,1536]{1,0:T(8,128)(2,1)} %bitcast.10, bf16[64,1536]{1,0:T(8,128)(2,1)} %bitcast.11), custom_call_target="tpu_custom_call" | custom-call | flops 6442450944 | bytes 16777216 | tf_op jit(solution)/shard_map/qkv/pallas_call | solution.py:254
  67.5 1.7 %copy.11 = bf16[4096,3,128]{2,0,1:T(8,128)(2,1)} copy(bf16[4096,3,128]{2,0,1:T(8,128)(2,1)S(1)} %bitcast.6) | data formatting | bytes 6291456
  69.2 1.0 %copy.12 = bf16[4096,1,128]{2,0,1:T(8,128)(2,1)} copy(bf16[4096,1,128]{2,0,1:T(8,128)(2,1)S(1)} %bitcast.8) | data formatting | bytes 2097152
  70.1 1.0 %copy.13 = bf16[4096,1,128]{2,0,1:T(8,128)(2,1)} copy(bf16[4096,1,128]{2,0,1:T(8,128)(2,1)S(1)} %bitcast.7) | data formatting | bytes 2097152

commit v2 on v1

--- a/solution.py
+++ b/solution.py
@@ -35,6 +35,10 @@
     across_other = (group, (1 - chip) * 2 + (1 - core))
     beside = (1 - group, member)
 
+    barrier = pltpu.get_barrier_semaphore()
+    for other in (across_other, across, beside, partner):
+        pl.semaphore_signal(barrier, inc=1, device_id=other, device_id_type=MESH)
+
     sources = [wk_hbm, wv_hbm] + [wq_hbm.at[h] for h in range(heads)]
 
     def piece_at(j, slot, depth_half=None):
@@ -60,9 +64,6 @@
     for load in x_loads:
         load.start()
 
-    barrier = pltpu.get_barrier_semaphore()
-    for other in (across, beside, across_other, partner):
-        pl.semaphore_signal(barrier, inc=1, device_id=other, device_id_type=MESH)
     pl.semaphore_wait(barrier, 4)
 
     def remote(src, dst, send, recv, device):
@@ -239,6 +240,20 @@
         copy.wait()
 
 
+def finish_kernel(q_ref, k_ref, v_ref, q_out, k_out, v_out, sems, *, cuts):
+    copies = []
+    for ref, out in ((q_ref, q_out), (k_ref, k_out), (v_ref, v_out)):
+        rows = ref.shape[1] // cuts
+        for h in range(ref.shape[0]):
+            for cut in range(cuts):
+                where = pl.ds(cut * rows, rows)
+                copies.append(pltpu.make_async_copy(ref.at[h, where], out.at[h, where], sems.at[len(copies)]))
+    for copy in copies:
+        copy.start()
+    for copy in copies:
+        copy.wait()
+
+
 def solution(mesh):
     def local_step(x_rows, norm_gain, w_q, w_k, w_v):
         n_rows, depth = x_rows.shape
@@ -276,6 +291,17 @@
             cost_estimate=pl.CostEstimate(flops=2 * n_rows * depth * 2048, bytes_accessed=16 * 1024 * 1024, transcendentals=0),
             name="qkv",
         )(*[pltpu.with_memory_space_constraint(a, pltpu.HBM) for a in (x_rows, norm_gain, w_q.transpose(1, 0, 2), w_k.T, w_v.T)])
+        cuts = 2
+        vmem = pl.BlockSpec(memory_space=pltpu.VMEM)
+        q, k, v = pl.pallas_call(
+            functools.partial(finish_kernel, cuts=cuts),
+            out_shape=tuple(jax.ShapeDtypeStruct(a.shape, a.dtype) for a in (q, k, v)),
+            in_specs=[vmem] * 3,
+            out_specs=(hbm,) * 3,
+            scratch_shapes=[dma((cuts * (heads + 2),))],
+            compiler_params=pltpu.CompilerParams(vmem_limit_bytes=16 * 1024 * 1024),
+            name="finish",
+        )(q, k, v)
         return q.transpose(1, 0, 2), k.transpose(1, 0, 2), v.transpose(1, 0, 2)
 
     return jax.shard_map(

time: 71.2 us -> 70 us (0.983)
  local copies, waits for them, and re-layouts: 3.61 us -> 0 us
  Pallas kernels: 66.9 us -> 69.3 us
    unnamed x3 -> x0, local copies, waits for them, and re-layouts: 3.61 us -> none
    pallas_call x0 -> x1, Pallas kernels: none -> 2.42 us  [local_step(): pl.pallas_call(functools.partial(finish_kernel, cuts=cuts), out_shape=tup...]
where the time goes in v2:
time: 70 us; the launch traced here: 69.9 us
  Pallas kernels  69.3 us (99%)
    pallas_call x1, Pallas kernels, local_step(): pl.pallas_call(functools.partial(qkv_kernel, norm_tile=norm_tile, dot_til...  66.9 us
    pallas_call x1, Pallas kernels, local_step(): pl.pallas_call(functools.partial(finish_kernel, cuts=cuts), out_shape=tup...  2.42 us

profile of v2, /device:TPU:1, one launch (start us, length us, event | category | flops | bytes accessed | tf_op | source)
XLA Modules:
  0.0 69.9 jit_solution(1235372680271821169)
XLA Ops:
  0.6 66.9 %qkv.1 = (bf16[3,4096,128]{2,1,0:T(8,128)(2,1)S(1)}, bf16[1,4096,128]{2,1,0:T(8,128)(2,1)S(1)}, bf16[1,4096,128]{2,1,0:T(8,128)(2,1)S(1)}) custom-call(bf16[1024,1536]{1,0:T(8,128)(2,1)} %x_hbm.1, f32[1536]{0:T(1024)} %gain_hbm.1, bf16[3,1536,128]{2,1,0:T(8,128)(2,1)} %bitcast.7, bf16[64,1536]{1,0:T(8,128)(2,1)} %bitcast.10, bf16[64,1536]{1,0:T(8,128)(2,1)} %bitcast.11), custom_call_target="tpu_custom_call" | custom-call | flops 6442450944 | bytes 16777216 | tf_op jit(solution)/shard_map/qkv/pallas_call | solution.py:269
  67.5 2.4 %finish.1 = (bf16[3,4096,128]{2,1,0:T(8,128)(2,1)}, bf16[1,4096,128]{2,1,0:T(8,128)(2,1)}, bf16[1,4096,128]{2,1,0:T(8,128)(2,1)}) custom-call(bf16[3,4096,128]{2,1,0:T(8,128)(2,1)S(1)} %get-tuple-element.9.q_ref, bf16[1,4096,128]{2,1,0:T(8,128)(2,1)S(1)} %get-tuple-element.10.k_ref, bf16[1,4096,128]{2,1,0:T(8,128)(2,1)S(1)} %get-tuple-element.11.v_ref), custom_call_target="tpu_custom_call" | custom-call | tf_op jit(solution)/shard_map/finish/pallas_call | solution.py:296

commit v3 on v2

--- a/solution.py
+++ b/solution.py
@@ -19,8 +19,9 @@
     rows_buf, gain_buf, wq_buf, wkv_buf, q_stage, kv_stage,
     x_sem, gain_sem, load_sem,
     part_send, part_recv, link_send, link_recv, core_send, core_recv, side_send, side_recv, last_send, last_recv,
+    middle_send, middle_recv, ready_sem,
     near_send, near_recv, far_send, far_recv, cross_send, cross_recv, pass_send, pass_recv,
-    *, norm_tile, dot_tile,
+    *, norm_tile, dot_tile, shift,
 ):
     n_rows, depth = rows_buf.shape
     heads = wq_hbm.shape[0]
@@ -36,10 +37,17 @@
     beside = (1 - group, member)
 
     barrier = pltpu.get_barrier_semaphore()
-    for other in (across_other, across, beside, partner):
+    for other in (across_other, across, partner):
         pl.semaphore_signal(barrier, inc=1, device_id=other, device_id_type=MESH)
 
+    @pl.when(group == 0)
+    def _():
+        pl.semaphore_signal(barrier, inc=1, device_id=beside, device_id_type=MESH)
+
     sources = [wk_hbm, wv_hbm] + [wq_hbm.at[h] for h in range(heads)]
+
+    last_head = pieces - 1
+    middle = pl.ds(half - shift, 2 * shift)
 
     def piece_at(j, slot, depth_half=None):
         if j < FIRST_HEAD:
@@ -49,22 +57,21 @@
             return wkv_buf.at[slot // 2, rows, pl.ds(pl.multiple_of(depth_half * half, half), half)]
         if depth_half is None:
             return wq_buf.at[slot, j - FIRST_HEAD]
+        if j == last_head:
+            start = pl.multiple_of(depth_half * (half + shift), shift)
+            return wq_buf.at[slot, j - FIRST_HEAD, pl.ds(start, half - shift)]
         return wq_buf.at[slot, j - FIRST_HEAD, pl.ds(pl.multiple_of(depth_half * half, half), half)]
 
     loads = [pltpu.make_async_copy(sources[j], piece_at(j, 0), load_sem.at[j]) for j in range(pieces)]
-    for load in loads:
+    for load in loads[:FIRST_HEAD]:
         load.start()
     gain_load = pltpu.make_async_copy(gain_hbm, gain_buf, gain_sem)
-    gain_load.start()
     n_tiles = n_rows // norm_tile
     x_loads = [
         pltpu.make_async_copy(x_hbm.at[pl.ds(i * norm_tile, norm_tile)], rows_buf.at[pl.ds(i * norm_tile, norm_tile)], x_sem.at[i])
         for i in range(n_tiles)
     ]
-    for load in x_loads:
-        load.start()
-
-    pl.semaphore_wait(barrier, 4)
+    pl.semaphore_wait(barrier, 3 + group)
 
     def remote(src, dst, send, recv, device):
         return pltpu.make_async_remote_copy(src_ref=src, dst_ref=dst, send_sem=send, recv_sem=recv, device_id=device, device_id_type=MESH)
@@ -77,6 +84,13 @@
         hand.append(remote(arrived, piece_at(j, 2 if j < FIRST_HEAD else 3, group), core_send.at[j], core_recv.at[j], partner))
         side.append(remote(arrived, arrived, side_send.at[j], side_recv.at[j], beside))
         last.append(remote(other_half, piece_at(j, 2 if j < FIRST_HEAD else 3, 1 - group), last_send.at[j], last_recv.at[j], partner))
+
+    def middle_at(slot):
+        return wq_buf.at[slot, heads - 1, middle]
+
+    middle_link = remote(middle_at(0), middle_at(2), middle_send.at[0], middle_recv.at[0], across)
+    middle_side = remote(middle_at(2), middle_at(2), middle_send.at[1], middle_recv.at[1], beside)
+    middle_hand = remote(middle_at(2), middle_at(3), middle_send.at[2], middle_recv.at[2], partner)
 
     my_rows = pl.ds(pl.multiple_of(member * n_rows, n_rows), n_rows)
     across_rows = pl.ds(pl.multiple_of(((1 - chip) * 2 + core) * n_rows, n_rows), n_rows)
@@ -92,10 +106,24 @@
         far.append(remote(q_stage.at[1, h], q_out.at[h, my_rows], far_send.at[2 + h], far_recv.at[2 + h], across))
         cross.append(remote(q_stage.at[2, h], q_out.at[h, my_rows], cross_send.at[h], cross_recv.at[h], across_other))
 
-    for j in range(pieces):
+    loads[0].wait()
+    link[0].start()
+    for load in loads[FIRST_HEAD:]:
+        load.start()
+    gain_load.start()
+    for load in x_loads:
+        load.start()
+    for j in range(1, pieces):
         loads[j].wait()
         link[j].start()
-        part[j].start()
+
+    @pl.when(group == 1)
+    def _():
+        middle_link.start()
+        pl.semaphore_signal(ready_sem, inc=1, device_id=beside, device_id_type=MESH)
+
+    for copy in part:
+        copy.start()
 
     gain_load.wait()
     chunks = depth // LANES
@@ -172,9 +200,25 @@
         side[j].wait_recv()
         last[j].start()
 
+    def from_middle():
+        @pl.when(group == 1)
+        def _():
+            middle_link.wait_recv()
+            middle_side.start()
+
+        @pl.when(group == 0)
+        def _():
+            middle_side.wait_recv()
+
+        middle_hand.start()
+
     def complete(j):
         hand[j].wait_recv()
         last[j].wait_recv()
+
+    @pl.when(group == 0)
+    def _():
+        pl.semaphore_wait(ready_sem, 1)
 
     from_link(K_PIECE)
     from_link(V_PIECE)
@@ -208,9 +252,11 @@
     staged_q(2, 3, 1)
     far[3].start()
     from_side(4)
+    from_middle()
     staged_q(1, 2, 2)
     cross[1].start()
     complete(4)
+    middle_hand.wait_recv()
     staged_q(2, 3, 2)
     far[4].start()
     for h in range(heads):
@@ -226,8 +272,14 @@
     passed[1].start()
     near[2 + heads - 1].start()
 
-    for copy in part + link + hand + side + last:
+    for copy in part + link + hand + side + last + [middle_hand]:
         copy.wait_send()
+
+    @pl.when(group == 1)
+    def _():
+        middle_link.wait_send()
+        middle_side.wait_send()
+
     for copy in near:
         copy.wait()
     for copy in passed:
@@ -267,7 +319,7 @@
         out_spec = pl.BlockSpec(memory_space=pltpu.VMEM)
         hbm = pl.BlockSpec(memory_space=pltpu.HBM)
         q, k, v = pl.pallas_call(
-            functools.partial(qkv_kernel, norm_tile=norm_tile, dot_tile=256),
+            functools.partial(qkv_kernel, norm_tile=norm_tile, dot_tile=256, shift=LANES),
             out_shape=(
                 jax.ShapeDtypeStruct((heads, all_rows, width), jnp.bfloat16),
                 jax.ShapeDtypeStruct((1, all_rows, width), jnp.bfloat16),
@@ -284,6 +336,7 @@
                 pltpu.VMEM((2, n_rows, width), jnp.bfloat16),
                 dma((4,)), dma(()), dma((pieces,)),
                 *[dma((pieces,)) for _ in range(10)],
+                dma((3,)), dma((3,)), pltpu.SemaphoreType.REGULAR,
                 dma((pieces,)), dma((pieces,)), dma((pieces,)), dma((pieces,)),
                 dma((heads,)), dma((heads,)), dma((2,)), dma((2,)),
             ],

time: 70 us -> 69.8 us (level); the launches traced: 69.9 us -> 69 us
  Pallas kernels: 69.3 us -> 68.3 us
    pallas_call x1, Pallas kernels: 66.9 us -> 65.9 us  [local_step(): pl.pallas_call(functools.partial(qkv_kernel, norm_tile=norm_tile, dot_til...]
where the time goes in v3:
time: 69.8 us; the launch traced here: 69 us
  Pallas kernels  68.3 us (98%)
    pallas_call x1, Pallas kernels, local_step(): pl.pallas_call(functools.partial(qkv_kernel, norm_tile=norm_tile, dot_til...  65.9 us
    pallas_call x1, Pallas kernels, local_step(): pl.pallas_call(functools.partial(finish_kernel, cuts=cuts), out_shape=tup...  2.42 us

profile of v3, /device:TPU:1, one launch (start us, length us, event | category | flops | bytes accessed | tf_op | source)
XLA Modules:
  0.0 69.0 jit_solution(14762838334736999031)
XLA Ops:
  0.6 65.9 %qkv.1 = (bf16[3,4096,128]{2,1,0:T(8,128)(2,1)S(1)}, bf16[1,4096,128]{2,1,0:T(8,128)(2,1)S(1)}, bf16[1,4096,128]{2,1,0:T(8,128)(2,1)S(1)}) custom-call(bf16[1024,1536]{1,0:T(8,128)(2,1)} %x_hbm.1, f32[1536]{0:T(1024)} %gain_hbm.1, bf16[3,1536,128]{2,1,0:T(8,128)(2,1)} %bitcast.7, bf16[64,1536]{1,0:T(8,128)(2,1)} %bitcast.10, bf16[64,1536]{1,0:T(8,128)(2,1)} %bitcast.11), custom_call_target="tpu_custom_call" | custom-call | flops 6442450944 | bytes 16777216 | tf_op jit(solution)/shard_map/qkv/pallas_call | solution.py:321
  66.5 2.4 %finish.1 = (bf16[3,4096,128]{2,1,0:T(8,128)(2,1)}, bf16[1,4096,128]{2,1,0:T(8,128)(2,1)}, bf16[1,4096,128]{2,1,0:T(8,128)(2,1)}) custom-call(bf16[3,4096,128]{2,1,0:T(8,128)(2,1)S(1)} %get-tuple-element.9.q_ref, bf16[1,4096,128]{2,1,0:T(8,128)(2,1)S(1)} %get-tuple-element.10.k_ref, bf16[1,4096,128]{2,1,0:T(8,128)(2,1)S(1)} %get-tuple-element.11.v_ref), custom_call_target="tpu_custom_call" | custom-call | tf_op jit(solution)/shard_map/finish/pallas_call | solution.py:349

commit v4 on v3

--- a/solution.py
+++ b/solution.py
@@ -19,7 +19,7 @@
     rows_buf, gain_buf, wq_buf, wkv_buf, q_stage, kv_stage,
     x_sem, gain_sem, load_sem,
     part_send, part_recv, link_send, link_recv, core_send, core_recv, side_send, side_recv, last_send, last_recv,
-    middle_send, middle_recv, ready_sem,
+    middle_send, middle_recv, ready_sem, pair_sem,
     near_send, near_recv, far_send, far_recv, cross_send, cross_recv, pass_send, pass_recv,
     *, norm_tile, dot_tile, shift,
 ):
@@ -37,7 +37,7 @@
     beside = (1 - group, member)
 
     barrier = pltpu.get_barrier_semaphore()
-    for other in (across_other, across, partner):
+    for other in (across, partner):
         pl.semaphore_signal(barrier, inc=1, device_id=other, device_id_type=MESH)
 
     @pl.when(group == 0)
@@ -71,7 +71,7 @@
         pltpu.make_async_copy(x_hbm.at[pl.ds(i * norm_tile, norm_tile)], rows_buf.at[pl.ds(i * norm_tile, norm_tile)], x_sem.at[i])
         for i in range(n_tiles)
     ]
-    pl.semaphore_wait(barrier, 3 + group)
+    pl.semaphore_wait(barrier, 2 + group)
 
     def remote(src, dst, send, recv, device):
         return pltpu.make_async_remote_copy(src_ref=src, dst_ref=dst, send_sem=send, recv_sem=recv, device_id=device, device_id_type=MESH)
@@ -116,6 +116,7 @@
     for j in range(1, pieces):
         loads[j].wait()
         link[j].start()
+    pl.semaphore_signal(pair_sem, inc=1, device_id=across, device_id_type=MESH)
 
     @pl.when(group == 1)
     def _():
@@ -215,6 +216,8 @@
     def complete(j):
         hand[j].wait_recv()
         last[j].wait_recv()
+
+    pl.semaphore_wait(pair_sem, 1)
 
     @pl.when(group == 0)
     def _():
@@ -336,7 +339,7 @@
                 pltpu.VMEM((2, n_rows, width), jnp.bfloat16),
                 dma((4,)), dma(()), dma((pieces,)),
                 *[dma((pieces,)) for _ in range(10)],
-                dma((3,)), dma((3,)), pltpu.SemaphoreType.REGULAR,
+                dma((3,)), dma((3,)), pltpu.SemaphoreType.REGULAR, pltpu.SemaphoreType.REGULAR,
                 dma((pieces,)), dma((pieces,)), dma((pieces,)), dma((pieces,)),
                 dma((heads,)), dma((heads,)), dma((2,)), dma((2,)),
             ],

time: 69.8 us -> 69.8 us (level)
  no operation moved by 1% of the time
where the time goes in v4:
time: 69.8 us; the launch traced here: 69 us
  Pallas kernels  68.3 us (98%)
    pallas_call x1, Pallas kernels, local_step(): pl.pallas_call(functools.partial(qkv_kernel, norm_tile=norm_tile, dot_til...  65.9 us
    pallas_call x1, Pallas kernels, local_step(): pl.pallas_call(functools.partial(finish_kernel, cuts=cuts), out_shape=tup...  2.42 us

profile of v4, /device:TPU:1, one launch (start us, length us, event | category | flops | bytes accessed | tf_op | source)
XLA Modules:
  0.0 69.0 jit_solution(353903776939456943)
XLA Ops:
  0.6 65.9 %qkv.1 = (bf16[3,4096,128]{2,1,0:T(8,128)(2,1)S(1)}, bf16[1,4096,128]{2,1,0:T(8,128)(2,1)S(1)}, bf16[1,4096,128]{2,1,0:T(8,128)(2,1)S(1)}) custom-call(bf16[1024,1536]{1,0:T(8,128)(2,1)} %x_hbm.1, f32[1536]{0:T(1024)} %gain_hbm.1, bf16[3,1536,128]{2,1,0:T(8,128)(2,1)} %bitcast.7, bf16[64,1536]{1,0:T(8,128)(2,1)} %bitcast.10, bf16[64,1536]{1,0:T(8,128)(2,1)} %bitcast.11), custom_call_target="tpu_custom_call" | custom-call | flops 6442450944 | bytes 16777216 | tf_op jit(solution)/shard_map/qkv/pallas_call | solution.py:324
  66.6 2.4 %finish.1 = (bf16[3,4096,128]{2,1,0:T(8,128)(2,1)}, bf16[1,4096,128]{2,1,0:T(8,128)(2,1)}, bf16[1,4096,128]{2,1,0:T(8,128)(2,1)}) custom-call(bf16[3,4096,128]{2,1,0:T(8,128)(2,1)S(1)} %get-tuple-element.9.q_ref, bf16[1,4096,128]{2,1,0:T(8,128)(2,1)S(1)} %get-tuple-element.10.k_ref, bf16[1,4096,128]{2,1,0:T(8,128)(2,1)S(1)} %get-tuple-element.11.v_ref), custom_call_target="tpu_custom_call" | custom-call | tf_op jit(solution)/shard_map/finish/pallas_call | solution.py:352

commit v5 on v0

v5 whole, which is shorter than its diff:
```python
import functools

import jax
import jax.numpy as jnp
from jax import lax
from jax.experimental import pallas as pl
from jax.experimental.pallas import tpu as pltpu
from jax.sharding import PartitionSpec as P

EPSILON = 1e-6
MESH = pl.DeviceIdType.MESH
LANES = 128
GATE = 1


def qkv_kernel(
    x_hbm, gain_hbm, wq_hbm, wk_hbm, wv_hbm,
    q_out, k_out, v_out,
    rows_buf, gain_buf, wq_buf, wkv_buf, stage, near_stage,
    x_sem, gain_sem, load_sem,
    part_send, part_recv, link_send, link_recv, side_send, side_recv, hand_send, hand_recv, last_send, last_recv,
    out_send, q_recv, kv_recv, relay_send, relay_recv, near_send, near_recv, pass_send, pass_recv,
    ready_sem, pair_sem,
    *, norm_tile, dot_tile, shift,
):
    n_rows, depth = rows_buf.shape
    heads = wq_hbm.shape[0]
    share = wk_hbm.shape[0]
    half = depth // 2
    pieces = 1 + heads

    group, member = lax.axis_index("dp"), lax.axis_index("tp")
    chip, core = member // 2, member % 2
    is_gate = core == GATE
    partner = (group, chip * 2 + (1 - core))
    across = (group, (1 - chip) * 2 + core)
    beside = (1 - group, member)

    def when(condition, act):
        pl.when(condition)(act)

    def signal(sem, device):
        pl.semaphore_signal(sem, inc=1, device_id=device, device_id_type=MESH)

    barrier = pltpu.get_barrier_semaphore()

    @pl.when(is_gate)
    def _():
        signal(barrier, across)
        when(group == 0, lambda: signal(barrier, beside))

    signal(barrier, partner)

    def kv_rows(owner):
        return pl.ds(pl.multiple_of(owner * 2 * share, 2 * share), 2 * share)

    k_load = pltpu.make_async_copy(wk_hbm, wkv_buf.at[0, pl.ds(pl.multiple_of(core * 2 * share, share), share)], load_sem.at[0])
    v_load = pltpu.make_async_copy(wv_hbm, wkv_buf.at[0, pl.ds(pl.multiple_of(core * 2 * share + share, share), share)], load_sem.at[1])
    q_loads = [pltpu.make_async_copy(wq_hbm.at[h], wq_buf.at[core, h], load_sem.at[2 + h]) for h in range(heads)]
    gain_load = pltpu.make_async_copy(gain_hbm, gain_buf, gain_sem)
    tiles = [pl.ds(i * norm_tile, norm_tile) for i in range(n_rows // norm_tile)]
    x_loads = [pltpu.make_async_copy(x_hbm.at[t], rows_buf.at[t], x_sem.at[i]) for i, t in enumerate(tiles)]
    k_load.start()
    v_load.start()
    for load in q_loads:
        load.start()

    pl.semaphore_wait(barrier, jnp.where(is_gate, 2 + group, 1))

    def remote(src, dst, send, recv, device):
        return pltpu.make_async_remote_copy(src_ref=src, dst_ref=dst, send_sem=send, recv_sem=recv, device_id=device, device_id_type=MESH)

    def piece(j, which, owner, depth_half=None):
        if depth_half is not None:
            extra = shift if (owner, j) == (0, heads) else 0
            cut = pl.ds(pl.multiple_of(depth_half * (half + extra), LANES), half - extra)
        if j == 0:
            return wkv_buf.at[which, kv_rows(owner)] if depth_half is None else wkv_buf.at[which, kv_rows(owner), cut]
        slot = wq_buf.at[which * 2 + owner, j - 1]
        return slot if depth_half is None else wq_buf.at[which * 2 + owner, j - 1, cut]

    part = [remote(piece(j, 0, core), piece(j, 0, core), part_send.at[j], part_recv.at[j], partner) for j in range(pieces)]
    link, side, hand, last = {}, {}, {}, {}
    for owner in range(2):
        for j in range(pieces):
            i = owner * pieces + j
            mine, theirs = piece(j, 1, owner, group), piece(j, 1, owner, 1 - group)
            link[owner, j] = remote(piece(j, 0, owner, group), mine, link_send.at[i], link_recv.at[i], across)
            side[owner, j] = remote(mine, mine, side_send.at[i], side_recv.at[i], beside)
            hand[owner, j] = remote(mine, mine, hand_send.at[i], hand_recv.at[i], partner)
            last[owner, j] = remote(theirs, theirs, last_send.at[i], last_recv.at[i], partner)
    extra = 2 * pieces
    middle = pl.ds(half - shift, 2 * shift)
    here, there = wq_buf.at[0, heads - 1, middle], wq_buf.at[2, heads - 1, middle]
    middle_link = remote(here, there, link_send.at[extra], link_recv.at[extra], across)
    middle_side = remote(there, there, side_send.at[extra], side_recv.at[extra], beside)
    middle_hand = remote(there, there, hand_send.at[extra], hand_recv.at[extra], partner)

    def block_of(owner, h):
        return 2 + owner * heads + h

    def rows_of(owner_chip, owner_core):
        return pl.ds(pl.multiple_of((owner_chip * 2 + owner_core) * n_rows, n_rows), n_rows)

    blocks = 2 + 2 * heads
    out = {}
    for r in range(2):
        rows = rows_of(chip, r)
        for i, ref in enumerate((k_out, v_out)):
            out[r, i] = remote(stage.at[r, i], ref.at[0, rows], out_send.at[r * blocks + i], kv_recv.at[r * 2 + i], across)
        for owner in range(2):
            for h in range(heads):
                b = block_of(owner, h)
                out[r, b] = remote(stage.at[r, b], q_out.at[h, rows], out_send.at[r * blocks + b], q_recv.at[r * heads + h],
                                   (group, (1 - chip) * 2 + owner))
    relay = [remote(stage.at[0, b], stage.at[0, b], relay_send.at[b], relay_recv.at[b], partner) for b in range(blocks)]
    passed = {}
    for r in range(2):
        rows = rows_of(1 - chip, r)
        for i, ref in enumerate((k_out, v_out)):
            passed[r, i] = remote(ref.at[0, rows], ref.at[0, rows], pass_send.at[r * 2 + i], pass_recv.at[r * 2 + i], partner)
    my_rows = rows_of(chip, core)
    near = [remote(ref.at[0, my_rows], ref.at[0, my_rows], near_send.at[i], near_recv.at[i], partner) for i, ref in enumerate((k_out, v_out))]
    near += [remote(near_stage.at[h], q_out.at[h, my_rows], near_send.at[2 + h], near_recv.at[2 + h], partner) for h in range(heads)]

    order = [(1, 0), (1, 1), (0, 0), (0, 1)] + [(owner, j) for j in range(2, pieces) for owner in (1, 0)]

    k_load.wait()
    v_load.wait()
    when(is_gate, link[order[0]].start)
    part[0].start()
    q_loads[0].wait()

    @pl.when(is_gate)
    def _():
        link[order[1]].start()
        signal(pair_sem, across)
        when(group == 1, lambda: signal(ready_sem, beside))

    gain_load.start()
    for load in x_loads:
        load.start()
    part[1].start()
    for j in range(2, pieces):
        q_loads[j - 1].wait()
        part[j].start()

    gain_load.wait()
    for load in x_loads:
        load.wait()
    chunks = depth // LANES
    sub = 64

    def norm_step(s, carry):
        here = pl.ds(pl.multiple_of(s * sub, sub), sub)
        total = jnp.zeros((sub, LANES), jnp.float32)
        for c in range(chunks):
            wide = rows_buf[here, c * LANES:(c + 1) * LANES].astype(jnp.float32)
            total = total + wide * wide
        scale = lax.rsqrt(jnp.sum(total, axis=-1, keepdims=True) / depth + EPSILON)
        for c in range(chunks):
            cols = slice(c * LANES, (c + 1) * LANES)
            wide = rows_buf[here, cols].astype(jnp.float32)
            rows_buf[here, cols] = (wide * scale * gain_buf[cols][None, :]).astype(jnp.bfloat16)
        return carry

    lax.fori_loop(0, n_rows // sub, norm_step, 0)

    for copy in part:
        copy.wait_recv()

    @pl.when(is_gate)
    def _():
        for key in order[2:]:
            link[key].start()
        when(group == 1, middle_link.start)
        pl.semaphore_wait(pair_sem, 1)
        when(group == 0, lambda: pl.semaphore_wait(ready_sem, 1))

    def over_tiles(step):
        lax.fori_loop(0, n_rows // dot_tile, lambda i, carry: (step(i * dot_tile), carry)[1], 0)

    def rows_at(start, base=0):
        return pl.ds(pl.multiple_of(base + start, dot_tile), dot_tile)

    def q_block(slot, h, store):
        def step(start):
            store(start, jnp.dot(rows_buf[rows_at(start), :], wq_buf[slot, h], preferred_element_type=jnp.float32).astype(jnp.bfloat16))
        over_tiles(step)

    def kv_block(which, store_k, store_v):
        def step(start):
            cut = [wkv_buf[which, i * share:(i + 1) * share, :] for i in (0, 2, 1, 3)]
            both = lax.dot_general(rows_buf[rows_at(start), :], jnp.concatenate(cut, axis=0), (((1,), (1,)), ((), ())),
                                   preferred_element_type=jnp.float32).astype(jnp.bfloat16)
            store_k(start, both[:, :LANES])
            store_v(start, both[:, LANES:])
        over_tiles(step)

    my_base = member * n_rows

    def own_q(h):
        def store(start, value):
            q_out[h, rows_at(start, my_base), :] = value
        q_block(core, h, store)

    def near_q(h):
        def store(start, value):
            near_stage[h, rows_at(start), :] = value
        q_block(1 - core, h, store)

    def far_q(owner, h):
        def store(start, value):
            stage[core, block_of(owner, h), rows_at(start), :] = value
        q_block(2 + owner, h, store)

    def own_kv():
        def store_k(start, value):
            k_out[0, rows_at(start, my_base), :] = value

        def store_v(start, value):
            v_out[0, rows_at(start, my_base), :] = value
        kv_block(0, store_k, store_v)

    def far_kv():
        def store_k(start, value):
            stage[core, 0, rows_at(start), :] = value

        def store_v(start, value):
            stage[core, 1, rows_at(start), :] = value
        kv_block(1, store_k, store_v)

    def send(b):
        when(is_gate, out[GATE, b].start)
        when(core != GATE, relay[b].start)

    def from_link(owner, j):
        @pl.when(is_gate)
        def _():
            link[owner, j].wait_recv()
            side[owner, j].start()
            hand[owner, j].start()

    def from_side(owner, j):
        @pl.when(is_gate)
        def _():
            side[owner, j].wait_recv()
            last[owner, j].start()

    def complete(owner, j):
        @pl.when(core != GATE)
        def _():
            hand[owner, j].wait_recv()
            last[owner, j].wait_recv()

    def from_middle():
        @pl.when(is_gate)
        def _():
            @pl.when(group == 1)
            def _():
                middle_link.wait_recv()
                middle_side.start()

            when(group == 0, middle_side.wait_recv)
            middle_hand.start()

    from_link(1, 0)
    own_kv()
    from_link(1, 1)
    own_q(0)
    near[0].start()
    near[1].start()
    from_side(1, 0)
    from_link(0, 0)
    own_q(1)
    from_side(1, 1)
    from_link(0, 1)
    complete(1, 1)
    far_q(1, 0)
    from_side(0, 0)
    from_link(1, 2)
    send(block_of(1, 0))
    complete(1, 0)
    complete(0, 0)
    far_kv()
    from_side(0, 1)
    from_link(0, 2)
    complete(0, 1)
    send(0)
    send(1)
    far_q(0, 0)
    from_side(1, 2)
    from_link(1, 3)
    send(block_of(0, 0))
    complete(1, 2)
    far_q(1, 1)
    from_side(0, 2)
    from_link(0, 3)
    send(block_of(1, 1))
    complete(0, 2)
    far_q(0, 1)
    from_side(1, 3)
    send(block_of(0, 1))
    complete(1, 3)
    far_q(1, 2)
    from_side(0, 3)
    from_middle()
    send(block_of(1, 2))
    complete(0, 3)
    when(core != GATE, middle_hand.wait_recv)
    far_q(0, 2)
    own_q(2)
    send(block_of(0, 2))
    for h in range(heads):
        near_q(h)
        if h:
            near[2 + h - 1].start()

    @pl.when(is_gate)
    def _():
        for b in range(blocks):
            relay[b].wait_recv()
            out[1 - GATE, b].start()

    near[2 + heads - 1].start()

    @pl.when(is_gate)
    def _():
        for r in (GATE, 1 - GATE):
            for i in range(2):
                out[r, i].wait_recv()
                passed[r, i].start()

    for copy in near:
        copy.wait()
    for copy in part:
        copy.wait_send()

    @pl.when(is_gate)
    def _():
        for copies in (link, side, hand, last, passed):
            for copy in copies.values():
                copy.wait_send()

        @pl.when(group == 1)
        def _():
            middle_link.wait_send()
            middle_side.wait_send()

        middle_hand.wait_send()

    @pl.when(core != GATE)
    def _():
        for copy in relay:
            copy.wait_send()
        for copy in passed.values():
            copy.wait_recv()

    for r in (GATE, 1 - GATE):
        for h in range(heads):
            out[r, block_of(0, h)].wait_recv()

    @pl.when(is_gate)
    def _():
        for copy in out.values():
            copy.wait_send()


def finish_kernel(q_ref, k_ref, v_ref, q_out, k_out, v_out, sems, *, cuts):
    copies = []
    for ref, out in ((q_ref, q_out), (k_ref, k_out), (v_ref, v_out)):
        rows = ref.shape[1] // cuts
        for h in range(ref.shape[0]):
            for cut in range(cuts):
                where = pl.ds(cut * rows, rows)
                copies.append(pltpu.make_async_copy(ref.at[h, where], out.at[h, where], sems.at[len(copies)]))
    for copy in copies:
        copy.start()
    for copy in copies:
        copy.wait()


def solution(mesh):
    def local_step(x_rows, norm_gain, w_q, w_k, w_v):
        n_rows, depth = x_rows.shape
        heads, width = w_q.shape[1:]
        share = w_k.shape[1]
        pieces = 1 + heads
        blocks = 2 + 2 * heads
        all_rows = mesh.shape["tp"] * n_rows
        dma = pltpu.SemaphoreType.DMA
        hbm = pl.BlockSpec(memory_space=pltpu.HBM)
        vmem = pl.BlockSpec(memory_space=pltpu.VMEM)
        inputs = (x_rows, norm_gain, w_q.transpose(1, 0, 2), w_k.T, w_v.T)
        results = tuple(jax.ShapeDtypeStruct((n, all_rows, width), jnp.bfloat16) for n in (heads, 1, 1))
        q, k, v = pl.pallas_call(
            functools.partial(qkv_kernel, norm_tile=n_rows // 4, dot_tile=256, shift=LANES),
            out_shape=results,
            in_specs=[hbm] * 5,
            out_specs=(vmem,) * 3,
            scratch_shapes=[
                pltpu.VMEM((n_rows, depth), jnp.bfloat16),
                pltpu.VMEM((depth,), jnp.float32),
                pltpu.VMEM((4, heads, depth, width), jnp.bfloat16),
                pltpu.VMEM((2, 4 * share, depth), jnp.bfloat16),
                pltpu.VMEM((2, blocks, n_rows, width), jnp.bfloat16),
                pltpu.VMEM((heads, n_rows, width), jnp.bfloat16),
                dma((4,)), dma(()), dma((2 + heads,)),
                dma((pieces,)), dma((pieces,)),
                *[dma((2 * pieces + 1,)) for _ in range(8)],
                dma((2 * blocks,)), dma((2 * heads,)), dma((4,)),
                dma((blocks,)), dma((blocks,)),
                dma((2 + heads,)), dma((2 + heads,)), dma((4,)), dma((4,)),
                pltpu.SemaphoreType.REGULAR, pltpu.SemaphoreType.REGULAR,
            ],
            compiler_params=pltpu.CompilerParams(collective_id=0, has_side_effects=True, vmem_limit_bytes=36 * 1024 * 1024),
            cost_estimate=pl.CostEstimate(flops=2 * n_rows * depth * 2048, bytes_accessed=16 * 1024 * 1024, transcendentals=0),
            name="qkv",
        )(*[pltpu.with_memory_space_constraint(a, pltpu.HBM) for a in inputs])
        cuts = 2
        q, k, v = pl.pallas_call(
            functools.partial(finish_kernel, cuts=cuts),
            out_shape=results,
            in_specs=[vmem] * 3,
            out_specs=(hbm,) * 3,
            scratch_shapes=[dma((cuts * (heads + 2),))],
            compiler_params=pltpu.CompilerParams(vmem_limit_bytes=16 * 1024 * 1024),
            name="finish",
        )(q, k, v)
        return q.transpose(1, 0, 2), k.transpose(1, 0, 2), v.transpose(1, 0, 2)

    return jax.shard_map(
        local_step, mesh=mesh,
        in_specs=(P(("dp", "tp"), None), P(None), P(None, "tp", None), P(None, "tp"), P(None, "tp")),
        out_specs=(P("dp", "tp", None), P("dp", "tp", None), P("dp", "tp", None)),
        check_vma=False,
    )
```

time: 129 us -> 70.4 us (0.55)
  waiting for transfers between devices: 82.3 us -> 0 us
  Pallas kernels: 0 us -> 69.6 us
  matrix products: 20.7 us -> 0 us
  between operations: 14.1 us -> 0.64 us
  other arithmetic: 7.63 us -> 0 us
  local copies, waits for them, and re-layouts: 2.79 us -> 0 us
    all_gather x1 -> x0, waiting for transfers between devices: 82.3 us -> none  [local_step(): gathered = lax.all_gather(normed, 'tp', axis=0, tiled=True)]
    pallas_call x0 -> x2, Pallas kernels: none -> 69.6 us  [the longest x1 67.2 us: local_step(): pl.pallas_call(functools.partial(qkv_kernel, norm_tile=n_rows // 4, dot_t...]
    dot_general x3 -> x0, matrix products: 20.7 us -> none  [the longest x1 8.59 us: local_step(): jnp.dot(gathered, w_k, preferred_element_type=jnp.float32)]
    reduce_sum x1 -> x0, other arithmetic: 2.72 us -> none  [local_step(): mean_sq = jnp.mean(x_wide * x_wide, axis=-1, keepdims=True)]
    dynamic_slice x2 -> x0, local copies, waits for them, and re-layouts: 2.62 us -> none  [head_pieces(): return jnp.roll(joined, member * piece.shape[1], axis=1)]
    concatenate x2 -> x0, other arithmetic: 2.46 us -> none  [head_pieces(): return jnp.roll(joined, member * piece.shape[1], axis=1)]
    convert_element_type x1 -> x0, other arithmetic: 2.45 us -> none  [local_step(): (x_wide * lax.rsqrt(mean_sq + EPSILON) * norm_gain).astype(jnp.bfloat16)]
  transfers between devices with their start and end apart: 3 -> 0, of which waited for: 1 -> 0; matrix products, arithmetic and copies ran while one was open for 11% -> 0% of each run, Pallas kernels for 0% -> 0%
where the time goes in v5:
time: 70.4 us; the launch traced here: 70.3 us
  Pallas kernels  69.6 us (99%)
    pallas_call x1, Pallas kernels, local_step(): pl.pallas_call(functools.partial(qkv_kernel, norm_tile=n_rows // 4, dot_t...  67.2 us
    pallas_call x1, Pallas kernels, local_step(): pl.pallas_call(functools.partial(finish_kernel, cuts=cuts), out_shape=res...  2.42 us

profile of v5, /device:TPU:1, one launch (start us, length us, event | category | flops | bytes accessed | tf_op | source)
XLA Modules:
  0.0 70.3 jit_solution(4203076560033428587)
XLA Ops:
  0.6 67.2 %qkv.1 = (bf16[3,4096,128]{2,1,0:T(8,128)(2,1)S(1)}, bf16[1,4096,128]{2,1,0:T(8,128)(2,1)S(1)}, bf16[1,4096,128]{2,1,0:T(8,128)(2,1)S(1)}) custom-call(bf16[1024,1536]{1,0:T(8,128)(2,1)} %x_hbm.1, f32[1536]{0:T(1024)} %gain_hbm.1, bf16[3,1536,128]{2,1,0:T(8,128)(2,1)} %bitcast.7, bf16[64,1536]{1,0:T(8,128)(2,1)} %bitcast.10, bf16[64,1536]{1,0:T(8,128)(2,1)} %bitcast.11), custom_call_target="tpu_custom_call" | custom-call | flops 6442450944 | bytes 16777216 | tf_op jit(solution)/shard_map/qkv/pallas_call | solution.py:396
  67.8 2.4 %finish.1 = (bf16[3,4096,128]{2,1,0:T(8,128)(2,1)}, bf16[1,4096,128]{2,1,0:T(8,128)(2,1)}, bf16[1,4096,128]{2,1,0:T(8,128)(2,1)}) custom-call(bf16[3,4096,128]{2,1,0:T(8,128)(2,1)S(1)} %get-tuple-element.9.q_ref, bf16[1,4096,128]{2,1,0:T(8,128)(2,1)S(1)} %get-tuple-element.10.k_ref, bf16[1,4096,128]{2,1,0:T(8,128)(2,1)S(1)} %get-tuple-element.11.v_ref), custom_call_target="tpu_custom_call" | custom-call | tf_op jit(solution)/shard_map/finish/pallas_call | solution.py:421

commit v6 on v4

--- a/solution.py
+++ b/solution.py
@@ -19,9 +19,9 @@
     rows_buf, gain_buf, wq_buf, wkv_buf, q_stage, kv_stage,
     x_sem, gain_sem, load_sem,
     part_send, part_recv, link_send, link_recv, core_send, core_recv, side_send, side_recv, last_send, last_recv,
-    middle_send, middle_recv, ready_sem, pair_sem,
+    middle_send, middle_recv, ready_sem, pair_sem, lent_buf, lent_sem,
     near_send, near_recv, far_send, far_recv, cross_send, cross_recv, pass_send, pass_recv,
-    *, norm_tile, dot_tile, shift,
+    *, norm_tile, dot_tile, shift, lent,
 ):
     n_rows, depth = rows_buf.shape
     heads = wq_hbm.shape[0]
@@ -58,7 +58,7 @@
         if depth_half is None:
             return wq_buf.at[slot, j - FIRST_HEAD]
         if j == last_head:
-            start = pl.multiple_of(depth_half * (half + shift), shift)
+            start = pl.multiple_of(depth_half * (half + shift), 32)
             return wq_buf.at[slot, j - FIRST_HEAD, pl.ds(start, half - shift)]
         return wq_buf.at[slot, j - FIRST_HEAD, pl.ds(pl.multiple_of(depth_half * half, half), half)]
 
@@ -106,6 +106,14 @@
         far.append(remote(q_stage.at[1, h], q_out.at[h, my_rows], far_send.at[2 + h], far_recv.at[2 + h], across))
         cross.append(remote(q_stage.at[2, h], q_out.at[h, my_rows], cross_send.at[h], cross_recv.at[h], across_other))
 
+    last_h = heads - 1
+    lent_rows, kept_rows = pl.ds(0, lent), pl.ds(lent, n_rows - lent)
+    my_kept = pl.ds(pl.multiple_of(member * n_rows + lent, lent), n_rows - lent)
+    partner_lent = pl.ds(pl.multiple_of((chip * 2 + 1 - core) * n_rows, n_rows), lent)
+    lend = remote(q_stage.at[2, last_h, lent_rows], lent_buf, lent_sem.at[0], lent_sem.at[1], partner)
+    cross_kept = remote(q_stage.at[2, last_h, kept_rows], q_out.at[last_h, my_kept], cross_send.at[last_h], cross_recv.at[last_h], across_other)
+    cross_lent = remote(lent_buf, q_out.at[last_h, partner_lent], lent_sem.at[2], lent_sem.at[3], across)
+
     loads[0].wait()
     link[0].start()
     for load in loads[FIRST_HEAD:]:
@@ -233,15 +241,14 @@
     near[1].start()
     from_link(2)
     from_side(V_PIECE)
-    own_q(0)
     complete(K_PIECE)
     complete(V_PIECE)
     far_kv()
-    own_q(1)
     far[0].start()
     far[1].start()
+    own_q(0)
     from_link(3)
-    own_q(2)
+    own_q(1)
     from_side(2)
     staged_q(1, 2, 0)
     from_link(4)
@@ -261,13 +268,25 @@
     complete(4)
     middle_hand.wait_recv()
     staged_q(2, 3, 2)
-    far[4].start()
+    own_q(2)
+
+    @pl.when(core == 0)
+    def _():
+        lend.start()
+        far[FIRST_HEAD + last_h].start()
+        cross_kept.start()
+
+    @pl.when(core == 1)
+    def _():
+        cross[last_h].start()
+        lend.wait_recv()
+        cross_lent.start()
+        far[FIRST_HEAD + last_h].start()
+
     for h in range(heads):
         part[FIRST_HEAD + h].wait_recv()
         staged_q(0, 1, h)
-        if h == 0:
-            cross[2].start()
-        else:
+        if h:
             near[2 + h - 1].start()
     far[0].wait_recv()
     passed[0].start()
@@ -291,8 +310,20 @@
         copy.wait_send()
         if j >= FIRST_HEAD:
             copy.wait_recv()
-    for copy in cross:
+    for copy in cross[:last_h]:
         copy.wait()
+
+    @pl.when(core == 0)
+    def _():
+        lend.wait_send()
+        cross_kept.wait_send()
+        cross[last_h].wait_recv()
+
+    @pl.when(core == 1)
+    def _():
+        cross[last_h].wait_send()
+        cross_lent.wait()
+        cross_kept.wait_recv()
 
 
 def finish_kernel(q_ref, k_ref, v_ref, q_out, k_out, v_out, sems, *, cuts):
@@ -319,10 +350,11 @@
         all_rows = members * n_rows
         dma = pltpu.SemaphoreType.DMA
         norm_tile = n_rows // 4
+        lent = 256
         out_spec = pl.BlockSpec(memory_space=pltpu.VMEM)
         hbm = pl.BlockSpec(memory_space=pltpu.HBM)
         q, k, v = pl.pallas_call(
-            functools.partial(qkv_kernel, norm_tile=norm_tile, dot_tile=256, shift=LANES),
+            functools.partial(qkv_kernel, norm_tile=norm_tile, dot_tile=256, shift=96, lent=lent),
             out_shape=(
                 jax.ShapeDtypeStruct((heads, all_rows, width), jnp.bfloat16),
                 jax.ShapeDtypeStruct((1, all_rows, width), jnp.bfloat16),
@@ -340,6 +372,7 @@
                 dma((4,)), dma(()), dma((pieces,)),
                 *[dma((pieces,)) for _ in range(10)],
                 dma((3,)), dma((3,)), pltpu.SemaphoreType.REGULAR, pltpu.SemaphoreType.REGULAR,
+                pltpu.VMEM((lent, width), jnp.bfloat16), dma((4,)),
                 dma((pieces,)), dma((pieces,)), dma((pieces,)), dma((pieces,)),
                 dma((heads,)), dma((heads,)), dma((2,)), dma((2,)),
             ],

time: 69.8 us -> 69.5 us (level)
  no operation moved by 1% of the time
where the time goes in v6:
time: 69.5 us; the launch traced here: 69.2 us
  Pallas kernels  68.6 us (99%)
    pallas_call x1, Pallas kernels, local_step(): pl.pallas_call(functools.partial(qkv_kernel, norm_tile=norm_tile, dot_til...  66.1 us
    pallas_call x1, Pallas kernels, local_step(): pl.pallas_call(functools.partial(finish_kernel, cuts=cuts), out_shape=tup...  2.42 us

profile of v6, /device:TPU:1, one launch (start us, length us, event | category | flops | bytes accessed | tf_op | source)
XLA Modules:
  0.0 69.2 jit_solution(1936126057542457768)
XLA Ops:
  0.6 66.1 %qkv.1 = (bf16[3,4096,128]{2,1,0:T(8,128)(2,1)S(1)}, bf16[1,4096,128]{2,1,0:T(8,128)(2,1)S(1)}, bf16[1,4096,128]{2,1,0:T(8,128)(2,1)S(1)}) custom-call(bf16[1024,1536]{1,0:T(8,128)(2,1)} %x_hbm.1, f32[1536]{0:T(1024)} %gain_hbm.1, bf16[3,1536,128]{2,1,0:T(8,128)(2,1)} %bitcast.7, bf16[64,1536]{1,0:T(8,128)(2,1)} %bitcast.10, bf16[64,1536]{1,0:T(8,128)(2,1)} %bitcast.11), custom_call_target="tpu_custom_call" | custom-call | flops 6442450944 | bytes 16777216 | tf_op jit(solution)/shard_map/qkv/pallas_call | solution.py:356
  66.8 2.4 %finish.1 = (bf16[3,4096,128]{2,1,0:T(8,128)(2,1)}, bf16[1,4096,128]{2,1,0:T(8,128)(2,1)}, bf16[1,4096,128]{2,1,0:T(8,128)(2,1)}) custom-call(bf16[3,4096,128]{2,1,0:T(8,128)(2,1)S(1)} %get-tuple-element.9.q_ref, bf16[1,4096,128]{2,1,0:T(8,128)(2,1)S(1)} %get-tuple-element.10.k_ref, bf16[1,4096,128]{2,1,0:T(8,128)(2,1)S(1)} %get-tuple-element.11.v_ref), custom_call_target="tpu_custom_call" | custom-call | tf_op jit(solution)/shard_map/finish/pallas_call | solution.py:385

commit v7 on v4

--- a/solution.py
+++ b/solution.py
@@ -15,7 +15,7 @@
 
 def qkv_kernel(
     x_hbm, gain_hbm, wq_hbm, wk_hbm, wv_hbm,
-    q_out, k_out, v_out,
+    q_out, k_out, v_out, late_out,
     rows_buf, gain_buf, wq_buf, wkv_buf, q_stage, kv_stage,
     x_sem, gain_sem, load_sem,
     part_send, part_recv, link_send, link_recv, core_send, core_recv, side_send, side_recv, last_send, last_recv,
@@ -58,7 +58,7 @@
         if depth_half is None:
             return wq_buf.at[slot, j - FIRST_HEAD]
         if j == last_head:
-            start = pl.multiple_of(depth_half * (half + shift), shift)
+            start = pl.multiple_of(depth_half * (half + shift), 16)
             return wq_buf.at[slot, j - FIRST_HEAD, pl.ds(start, half - shift)]
         return wq_buf.at[slot, j - FIRST_HEAD, pl.ds(pl.multiple_of(depth_half * half, half), half)]
 
@@ -103,7 +103,7 @@
     cross = []
     for h in range(heads):
         near.append(remote(q_stage.at[0, h], q_out.at[h, my_rows], near_send.at[2 + h], near_recv.at[2 + h], partner))
-        far.append(remote(q_stage.at[1, h], q_out.at[h, my_rows], far_send.at[2 + h], far_recv.at[2 + h], across))
+        far.append(remote(q_stage.at[1, 0] if h == 0 else late_out.at[h - 1], q_out.at[h, my_rows], far_send.at[2 + h], far_recv.at[2 + h], across))
         cross.append(remote(q_stage.at[2, h], q_out.at[h, my_rows], cross_send.at[h], cross_recv.at[h], across_other))
 
     loads[0].wait()
@@ -180,6 +180,11 @@
             q_stage[stage, h, rows_at(start), :] = value
         q_block(slot, h, store)
 
+    def late_q(h):
+        def store(start, value):
+            late_out[h - 1, rows_at(start), :] = value
+        q_block(2, h, store)
+
     def own_kv():
         def store(start, value):
             k_out[0, own_rows_at(start), :] = value[:, :LANES]
@@ -233,15 +238,14 @@
     near[1].start()
     from_link(2)
     from_side(V_PIECE)
-    own_q(0)
     complete(K_PIECE)
     complete(V_PIECE)
     far_kv()
-    own_q(1)
     far[0].start()
     far[1].start()
+    own_q(0)
     from_link(3)
-    own_q(2)
+    own_q(1)
     from_side(2)
     staged_q(1, 2, 0)
     from_link(4)
@@ -249,25 +253,29 @@
     staged_q(2, 3, 0)
     far[2].start()
     from_side(3)
-    staged_q(1, 2, 1)
-    cross[0].start()
     complete(3)
     staged_q(2, 3, 1)
-    far[3].start()
+    cross[0].start()
+    late_q(1)
     from_side(4)
     from_middle()
-    staged_q(1, 2, 2)
     cross[1].start()
     complete(4)
     middle_hand.wait_recv()
     staged_q(2, 3, 2)
-    far[4].start()
+    late_q(2)
+    cross[2].start()
+    own_q(2)
+
+    @pl.when(core == 0)
+    def _():
+        for copy in far[FIRST_HEAD + 1:]:
+            copy.start()
+
     for h in range(heads):
         part[FIRST_HEAD + h].wait_recv()
         staged_q(0, 1, h)
-        if h == 0:
-            cross[2].start()
-        else:
+        if h:
             near[2 + h - 1].start()
     far[0].wait_recv()
     passed[0].start()
@@ -283,30 +291,79 @@
         middle_link.wait_send()
         middle_side.wait_send()
 
-    for copy in near:
+    for copy in near + passed + cross:
         copy.wait()
-    for copy in passed:
+    for copy in far[:FIRST_HEAD]:
+        copy.wait_send()
+    far[FIRST_HEAD].wait()
+
+    @pl.when(core == 0)
+    def _():
+        for copy in far[FIRST_HEAD + 1:]:
+            copy.wait()
+
+
+def finish_kernel(q_ref, k_ref, v_ref, q_out, k_out, v_out, sems):
+    member = lax.axis_index("tp")
+    chip, core = member // 2, member % 2
+    n_rows = q_ref.shape[1] // 4
+    here, there = [], []
+    for ref, out in ((q_ref, q_out), (k_ref, k_out), (v_ref, v_out)):
+        for h in range(ref.shape[0]):
+            for cut in range(4):
+                where = pl.ds(pl.multiple_of(((3 - 2 * chip + cut + 1) % 4) * n_rows, n_rows), n_rows)
+                copy = pltpu.make_async_copy(ref.at[h, where], out.at[h, where], sems.at[len(here) + len(there)])
+                (there if cut == 3 and ref is q_ref and h else here).append(copy)
+
+    for copy in here:
+        copy.start()
+
+    @pl.when(core == 0)
+    def _():
+        for copy in there:
+            copy.start()
+
+    for copy in here:
         copy.wait()
-    for j, copy in enumerate(far):
-        copy.wait_send()
-        if j >= FIRST_HEAD:
-            copy.wait_recv()
-    for copy in cross:
-        copy.wait()
-
-
-def finish_kernel(q_ref, k_ref, v_ref, q_out, k_out, v_out, sems, *, cuts):
-    copies = []
-    for ref, out in ((q_ref, q_out), (k_ref, k_out), (v_ref, v_out)):
-        rows = ref.shape[1] // cuts
-        for h in range(ref.shape[0]):
-            for cut in range(cuts):
-                where = pl.ds(cut * rows, rows)
-                copies.append(pltpu.make_async_copy(ref.at[h, where], out.at[h, where], sems.at[len(copies)]))
-    for copy in copies:
-        copy.start()
-    for copy in copies:
-        copy.wait()
+
+    @pl.when(core == 0)
+    def _():
+        for copy in there:
+            copy.wait()
+
+
+def late_kernel(after_ref, late_out, late_in, send_sem, recv_sem):
+    group, member = lax.axis_index("dp"), lax.axis_index("tp")
+
+    @pl.when(member % 2 == 1)
+    def _():
+        across = (group, (member + 2) % 4)
+        barrier = pltpu.get_barrier_semaphore()
+        pl.semaphore_signal(barrier, inc=1, device_id=across, device_id_type=MESH)
+        pl.semaphore_wait(barrier, 1)
+        copies = [
+            pltpu.make_async_remote_copy(src_ref=late_out.at[i], dst_ref=late_in.at[i], send_sem=send_sem.at[i], recv_sem=recv_sem.at[i],
+                                         device_id=across, device_id_type=MESH)
+            for i in range(late_out.shape[0])
+        ]
+        for copy in copies:
+            copy.start()
+        for copy in copies:
+            copy.wait()
+
+
+def patch_kernel(before_ref, late_ref, q_out, sems):
+    member = lax.axis_index("tp")
+    n_rows = late_ref.shape[1]
+
+    @pl.when(member % 2 == 1)
+    def _():
+        where = pl.ds(pl.multiple_of(((member + 2) % 4) * n_rows, n_rows), n_rows)
+        copies = [pltpu.make_async_copy(late_ref.at[i], q_out.at[1 + i, where], sems.at[i]) for i in range(late_ref.shape[0])]
+        for copy in copies:
+            copy.start()
+        for copy in copies:
+            copy.wait()
 
 
 def solution(mesh):
@@ -319,17 +376,15 @@
         all_rows = members * n_rows
         dma = pltpu.SemaphoreType.DMA
         norm_tile = n_rows // 4
-        out_spec = pl.BlockSpec(memory_space=pltpu.VMEM)
+        vmem = pl.BlockSpec(memory_space=pltpu.VMEM)
+        results = tuple(jax.ShapeDtypeStruct((n, all_rows, width), jnp.bfloat16) for n in (heads, 1, 1))
         hbm = pl.BlockSpec(memory_space=pltpu.HBM)
-        q, k, v = pl.pallas_call(
-            functools.partial(qkv_kernel, norm_tile=norm_tile, dot_tile=256, shift=LANES),
-            out_shape=(
-                jax.ShapeDtypeStruct((heads, all_rows, width), jnp.bfloat16),
-                jax.ShapeDtypeStruct((1, all_rows, width), jnp.bfloat16),
-                jax.ShapeDtypeStruct((1, all_rows, width), jnp.bfloat16),
-            ),
+        late_shape = jax.ShapeDtypeStruct((heads - 1, n_rows, width), jnp.bfloat16)
+        q, k, v, late = pl.pallas_call(
+            functools.partial(qkv_kernel, norm_tile=norm_tile, dot_tile=256, shift=80),
+            out_shape=results + (late_shape,),
             in_specs=[hbm] * 5,
-            out_specs=(out_spec,) * 3,
+            out_specs=(vmem,) * 4,
             scratch_shapes=[
                 pltpu.VMEM((n_rows, depth), jnp.bfloat16),
                 pltpu.VMEM((depth,), jnp.float32),
@@ -347,17 +402,34 @@
             cost_estimate=pl.CostEstimate(flops=2 * n_rows * depth * 2048, bytes_accessed=16 * 1024 * 1024, transcendentals=0),
             name="qkv",
         )(*[pltpu.with_memory_space_constraint(a, pltpu.HBM) for a in (x_rows, norm_gain, w_q.transpose(1, 0, 2), w_k.T, w_v.T)])
-        cuts = 2
-        vmem = pl.BlockSpec(memory_space=pltpu.VMEM)
         q, k, v = pl.pallas_call(
-            functools.partial(finish_kernel, cuts=cuts),
-            out_shape=tuple(jax.ShapeDtypeStruct(a.shape, a.dtype) for a in (q, k, v)),
+            finish_kernel,
+            out_shape=results,
             in_specs=[vmem] * 3,
             out_specs=(hbm,) * 3,
-            scratch_shapes=[dma((cuts * (heads + 2),))],
+            scratch_shapes=[dma((4 * (heads + 2),))],
             compiler_params=pltpu.CompilerParams(vmem_limit_bytes=16 * 1024 * 1024),
             name="finish",
         )(q, k, v)
+        late = pl.pallas_call(
+            late_kernel,
+            out_shape=late_shape,
+            in_specs=[hbm, vmem],
+            out_specs=vmem,
+            scratch_shapes=[dma((heads - 1,)), dma((heads - 1,))],
+            compiler_params=pltpu.CompilerParams(collective_id=1, has_side_effects=True, vmem_limit_bytes=16 * 1024 * 1024),
+            name="late",
+        )(pltpu.with_memory_space_constraint(q, pltpu.HBM), late)
+        q = pl.pallas_call(
+            patch_kernel,
+            out_shape=results[0],
+            in_specs=[hbm, vmem],
+            out_specs=hbm,
+            scratch_shapes=[dma((heads - 1,))],
+            input_output_aliases={0: 0},
+            compiler_params=pltpu.CompilerParams(vmem_limit_bytes=16 * 1024 * 1024),
+            name="patch",
+        )(q, late)
         return q.transpose(1, 0, 2), k.transpose(1, 0, 2), v.transpose(1, 0, 2)
 
     return jax.shard_map(

time: 69.8 us -> 67 us (0.960)
  Pallas kernels: 68.3 us -> 66.2 us
    pallas_call x1, Pallas kernels: 65.9 us -> 55 us  [local_step(): pl.pallas_call(functools.partial(qkv_kernel, norm_tile=norm_tile, dot_til...]
    pallas_call x1 -> x3, Pallas kernels: 2.42 us -> 11.3 us  [the longest x1 8.09 us: local_step(): pl.pallas_call(late_kernel, out_shape=late_shape, in_specs=[hbm, vmem], o...]
where the time goes in v7:
time: 67 us; the launch traced here: 66.9 us
  Pallas kernels  66.2 us (99%)
    pallas_call x1, Pallas kernels, local_step(): pl.pallas_call(functools.partial(qkv_kernel, norm_tile=norm_tile, dot_til...  55 us
    pallas_call x1, Pallas kernels, local_step(): pl.pallas_call(late_kernel, out_shape=late_shape, in_specs=[hbm, vmem], o...  8.09 us
    pallas_call x1, Pallas kernels, local_step(): pl.pallas_call(finish_kernel, out_shape=results, in_specs=[vmem] * 3, out...  2.35 us

profile of v7, /device:TPU:1, one launch (start us, length us, event | category | flops | bytes accessed | tf_op | source)
XLA Modules:
  0.0 66.9 jit_solution(10857990528929634675)
XLA Ops:
  0.6 55.0 %qkv.1 = (bf16[3,4096,128]{2,1,0:T(8,128)(2,1)S(1)}, bf16[1,4096,128]{2,1,0:T(8,128)(2,1)S(1)}, bf16[1,4096,128]{2,1,0:T(8,128)(2,1)S(1)}, bf16[2,1024,128]{2,1,0:T(8,128)(2,1)S(1)}) custom-call(bf16[1024,1536]{1,0:T(8,128)(2,1)} %x_hbm.1, f32[1536]{0:T(1024)} %gain_hbm.1, bf16[3,1536,128]{2,1,0:T(8,128)(2,1)} %bitcast.7, bf16[64,1536]{1,0:T(8,128)(2,1)} %bitcast.10, ...), custom_call_target="tpu_custom_call" | custom-call | flops 6442450944 | bytes 16777216 | tf_op jit(solution)/shard_map/qkv/pallas_call | solution.py:383
  55.6 2.4 %finish.1 = (bf16[3,4096,128]{2,1,0:T(8,128)(2,1)}, bf16[1,4096,128]{2,1,0:T(8,128)(2,1)}, bf16[1,4096,128]{2,1,0:T(8,128)(2,1)}) custom-call(bf16[3,4096,128]{2,1,0:T(8,128)(2,1)S(1)} %get-tuple-element.10.q_ref, bf16[1,4096,128]{2,1,0:T(8,128)(2,1)S(1)} %get-tuple-element.11.k_ref, bf16[1,4096,128]{2,1,0:T(8,128)(2,1)S(1)} %get-tuple-element.12.v_ref), custom_call_target="tpu_custom_call" | custom-call | tf_op jit(solution)/shard_map/finish/pallas_call | solution.py:405
  58.0 8.1 %late.1.late_ref = bf16[2,1024,128]{2,1,0:T(8,128)(2,1)S(1)} custom-call(bf16[3,4096,128]{2,1,0:T(8,128)(2,1)} %get-tuple-element.13.after_ref.before_ref, bf16[2,1024,128]{2,1,0:T(8,128)(2,1)S(1)} %get-tuple-element.14.late_out), custom_call_target="tpu_custom_call" | custom-call | tf_op jit(solution)/shard_map/late/pallas_call | solution.py:414
  66.0 0.8 %patch.1 = bf16[3,4096,128]{2,1,0:T(8,128)(2,1)} custom-call(bf16[3,4096,128]{2,1,0:T(8,128)(2,1)} %get-tuple-element.13.after_ref.before_ref, bf16[2,1024,128]{2,1,0:T(8,128)(2,1)S(1)} %late.1.late_ref), custom_call_target="tpu_custom_call", output_to_operand_aliasing={{}: (0, {})} | custom-call | tf_op jit(solution)/shard_map/patch/pallas_call | solution.py:423

commit v8 on v7

--- a/solution.py
+++ b/solution.py
@@ -36,14 +36,6 @@
     across_other = (group, (1 - chip) * 2 + (1 - core))
     beside = (1 - group, member)
 
-    barrier = pltpu.get_barrier_semaphore()
-    for other in (across, partner):
-        pl.semaphore_signal(barrier, inc=1, device_id=other, device_id_type=MESH)
-
-    @pl.when(group == 0)
-    def _():
-        pl.semaphore_signal(barrier, inc=1, device_id=beside, device_id_type=MESH)
-
     sources = [wk_hbm, wv_hbm] + [wq_hbm.at[h] for h in range(heads)]
 
     last_head = pieces - 1
@@ -62,9 +54,23 @@
             return wq_buf.at[slot, j - FIRST_HEAD, pl.ds(start, half - shift)]
         return wq_buf.at[slot, j - FIRST_HEAD, pl.ds(pl.multiple_of(depth_half * half, half), half)]
 
-    loads = [pltpu.make_async_copy(sources[j], piece_at(j, 0), load_sem.at[j]) for j in range(pieces)]
-    for load in loads[:FIRST_HEAD]:
+    firsts, rests = [], []
+    for j in range(FIRST_HEAD):
+        for copies, which, sem in ((firsts, group, j), (rests, 1 - group, pieces + j)):
+            cols = pl.ds(pl.multiple_of(which * half, half), half)
+            copies.append(pltpu.make_async_copy(sources[j].at[:, cols], piece_at(j, 0, which), load_sem.at[sem]))
+    head_loads = [pltpu.make_async_copy(sources[j], piece_at(j, 0), load_sem.at[j]) for j in range(FIRST_HEAD, pieces)]
+    for load in firsts:
         load.start()
+
+    barrier = pltpu.get_barrier_semaphore()
+    for other in (across, partner):
+        pl.semaphore_signal(barrier, inc=1, device_id=other, device_id_type=MESH)
+
+    @pl.when(group == 0)
+    def _():
+        pl.semaphore_signal(barrier, inc=1, device_id=beside, device_id_type=MESH)
+
     gain_load = pltpu.make_async_copy(gain_hbm, gain_buf, gain_sem)
     n_tiles = n_rows // norm_tile
     x_loads = [
@@ -106,16 +112,17 @@
         far.append(remote(q_stage.at[1, 0] if h == 0 else late_out.at[h - 1], q_out.at[h, my_rows], far_send.at[2 + h], far_recv.at[2 + h], across))
         cross.append(remote(q_stage.at[2, h], q_out.at[h, my_rows], cross_send.at[h], cross_recv.at[h], across_other))
 
-    loads[0].wait()
+    firsts[0].wait()
     link[0].start()
-    for load in loads[FIRST_HEAD:]:
+    for load in head_loads[:1] + rests + head_loads[1:] + [gain_load] + x_loads:
         load.start()
-    gain_load.start()
-    for load in x_loads:
-        load.start()
-    for j in range(1, pieces):
-        loads[j].wait()
+    firsts[1].wait()
+    link[1].start()
+    for j in range(FIRST_HEAD, pieces):
+        head_loads[j - FIRST_HEAD].wait()
         link[j].start()
+    for load in rests:
+        load.wait()
     pl.semaphore_signal(pair_sem, inc=1, device_id=across, device_id_type=MESH)
 
     @pl.when(group == 1)
@@ -392,7 +399,7 @@
                 pltpu.VMEM((2, 4 * share, depth), jnp.bfloat16),
                 pltpu.VMEM((3, heads, n_rows, width), jnp.bfloat16),
                 pltpu.VMEM((2, n_rows, width), jnp.bfloat16),
-                dma((4,)), dma(()), dma((pieces,)),
+                dma((4,)), dma(()), dma((pieces + FIRST_HEAD,)),
                 *[dma((pieces,)) for _ in range(10)],
                 dma((3,)), dma((3,)), pltpu.SemaphoreType.REGULAR, pltpu.SemaphoreType.REGULAR,
                 dma((pieces,)), dma((pieces,)), dma((pieces,)), dma((pieces,)),

time: 67 us -> 67 us (level)
  no operation moved by 1% of the time
where the time goes in v8:
time: 67 us; the launch traced here: 66.8 us
  Pallas kernels  66.2 us (99%)
    pallas_call x1, Pallas kernels, local_step(): pl.pallas_call(functools.partial(qkv_kernel, norm_tile=norm_tile, dot_til...  54.9 us
    pallas_call x1, Pallas kernels, local_step(): pl.pallas_call(late_kernel, out_shape=late_shape, in_specs=[hbm, vmem], o...  8.09 us
    pallas_call x1, Pallas kernels, local_step(): pl.pallas_call(finish_kernel, out_shape=results, in_specs=[vmem] * 3, out...  2.35 us

profile of v8, /device:TPU:1, one launch (start us, length us, event | category | flops | bytes accessed | tf_op | source)
XLA Modules:
  0.0 66.8 jit_solution(648540024105217846)
XLA Ops:
  0.6 54.9 %qkv.1 = (bf16[3,4096,128]{2,1,0:T(8,128)(2,1)S(1)}, bf16[1,4096,128]{2,1,0:T(8,128)(2,1)S(1)}, bf16[1,4096,128]{2,1,0:T(8,128)(2,1)S(1)}, bf16[2,1024,128]{2,1,0:T(8,128)(2,1)S(1)}) custom-call(bf16[1024,1536]{1,0:T(8,128)(2,1)} %x_hbm.1, f32[1536]{0:T(1024)} %gain_hbm.1, bf16[3,1536,128]{2,1,0:T(8,128)(2,1)} %bitcast.7, bf16[64,1536]{1,0:T(8,128)(2,1)} %bitcast.10, ...), custom_call_target="tpu_custom_call" | custom-call | flops 6442450944 | bytes 16777216 | tf_op jit(solution)/shard_map/qkv/pallas_call | solution.py:390
  55.6 2.4 %finish.1 = (bf16[3,4096,128]{2,1,0:T(8,128)(2,1)}, bf16[1,4096,128]{2,1,0:T(8,128)(2,1)}, bf16[1,4096,128]{2,1,0:T(8,128)(2,1)}) custom-call(bf16[3,4096,128]{2,1,0:T(8,128)(2,1)S(1)} %get-tuple-element.10.q_ref, bf16[1,4096,128]{2,1,0:T(8,128)(2,1)S(1)} %get-tuple-element.11.k_ref, bf16[1,4096,128]{2,1,0:T(8,128)(2,1)S(1)} %get-tuple-element.12.v_ref), custom_call_target="tpu_custom_call" | custom-call | tf_op jit(solution)/shard_map/finish/pallas_call | solution.py:412
  57.9 8.1 %late.1.late_ref = bf16[2,1024,128]{2,1,0:T(8,128)(2,1)S(1)} custom-call(bf16[3,4096,128]{2,1,0:T(8,128)(2,1)} %get-tuple-element.13.after_ref.before_ref, bf16[2,1024,128]{2,1,0:T(8,128)(2,1)S(1)} %get-tuple-element.14.late_out), custom_call_target="tpu_custom_call" | custom-call | tf_op jit(solution)/shard_map/late/pallas_call | solution.py:421
  66.0 0.8 %patch.1 = bf16[3,4096,128]{2,1,0:T(8,128)(2,1)} custom-call(bf16[3,4096,128]{2,1,0:T(8,128)(2,1)} %get-tuple-element.13.after_ref.before_ref, bf16[2,1024,128]{2,1,0:T(8,128)(2,1)S(1)} %late.1.late_ref), custom_call_target="tpu_custom_call", output_to_operand_aliasing={{}: (0, {})} | custom-call | tf_op jit(solution)/shard_map/patch/pallas_call | solution.py:430

commit v9 on v8

--- a/solution.py
+++ b/solution.py
@@ -258,7 +258,11 @@
     from_link(4)
     complete(2)
     staged_q(2, 3, 0)
-    far[2].start()
+
+    @pl.when(core == 1)
+    def _():
+        far[FIRST_HEAD].start()
+
     from_side(3)
     complete(3)
     staged_q(2, 3, 1)
@@ -276,7 +280,7 @@
 
     @pl.when(core == 0)
     def _():
-        for copy in far[FIRST_HEAD + 1:]:
+        for copy in far[FIRST_HEAD:]:
             copy.start()
 
     for h in range(heads):

time: 67 us -> 67.3 us (level)
    pallas_call x1, Pallas kernels: 54.9 us -> 52.4 us  [local_step(): pl.pallas_call(functools.partial(qkv_kernel, norm_tile=norm_tile, dot_til...]
    pallas_call x1, Pallas kernels: 8.09 us -> 10.5 us  [local_step(): pl.pallas_call(late_kernel, out_shape=late_shape, in_specs=[hbm, vmem], o...]
where the time goes in v9:
time: 67.3 us; the launch traced here: 66.8 us
  Pallas kernels  66.1 us (98%)
    pallas_call x1, Pallas kernels, local_step(): pl.pallas_call(functools.partial(qkv_kernel, norm_tile=norm_tile, dot_til...  52.4 us
    pallas_call x1, Pallas kernels, local_step(): pl.pallas_call(late_kernel, out_shape=late_shape, in_specs=[hbm, vmem], o...  10.5 us
    pallas_call x1, Pallas kernels, local_step(): pl.pallas_call(finish_kernel, out_shape=results, in_specs=[vmem] * 3, out...  2.35 us

profile of v9, /device:TPU:1, one launch (start us, length us, event | category | flops | bytes accessed | tf_op | source)
XLA Modules:
  0.0 66.8 jit_solution(9969763140849079950)
XLA Ops:
  0.6 52.4 %qkv.1 = (bf16[3,4096,128]{2,1,0:T(8,128)(2,1)S(1)}, bf16[1,4096,128]{2,1,0:T(8,128)(2,1)S(1)}, bf16[1,4096,128]{2,1,0:T(8,128)(2,1)S(1)}, bf16[2,1024,128]{2,1,0:T(8,128)(2,1)S(1)}) custom-call(bf16[1024,1536]{1,0:T(8,128)(2,1)} %x_hbm.1, f32[1536]{0:T(1024)} %gain_hbm.1, bf16[3,1536,128]{2,1,0:T(8,128)(2,1)} %bitcast.7, bf16[64,1536]{1,0:T(8,128)(2,1)} %bitcast.10, ...), custom_call_target="tpu_custom_call" | custom-call | flops 6442450944 | bytes 16777216 | tf_op jit(solution)/shard_map/qkv/pallas_call | solution.py:394
  53.1 2.4 %finish.1 = (bf16[3,4096,128]{2,1,0:T(8,128)(2,1)}, bf16[1,4096,128]{2,1,0:T(8,128)(2,1)}, bf16[1,4096,128]{2,1,0:T(8,128)(2,1)}) custom-call(bf16[3,4096,128]{2,1,0:T(8,128)(2,1)S(1)} %get-tuple-element.10.q_ref, bf16[1,4096,128]{2,1,0:T(8,128)(2,1)S(1)} %get-tuple-element.11.k_ref, bf16[1,4096,128]{2,1,0:T(8,128)(2,1)S(1)} %get-tuple-element.12.v_ref), custom_call_target="tpu_custom_call" | custom-call | tf_op jit(solution)/shard_map/finish/pallas_call | solution.py:416
  55.4 10.5 %late.1.late_ref = bf16[2,1024,128]{2,1,0:T(8,128)(2,1)S(1)} custom-call(bf16[3,4096,128]{2,1,0:T(8,128)(2,1)} %get-tuple-element.13.after_ref.before_ref, bf16[2,1024,128]{2,1,0:T(8,128)(2,1)S(1)} %get-tuple-element.14.late_out), custom_call_target="tpu_custom_call" | custom-call | tf_op jit(solution)/shard_map/late/pallas_call | solution.py:425
  65.9 0.8 %patch.1 = bf16[3,4096,128]{2,1,0:T(8,128)(2,1)} custom-call(bf16[3,4096,128]{2,1,0:T(8,128)(2,1)} %get-tuple-element.13.after_ref.before_ref, bf16[2,1024,128]{2,1,0:T(8,128)(2,1)S(1)} %late.1.late_ref), custom_call_target="tpu_custom_call", output_to_operand_aliasing={{}: (0, {})} | custom-call | tf_op jit(solution)/shard_map/patch/pallas_call | solution.py:434

commit v10 on v9

--- a/solution.py
+++ b/solution.py
@@ -19,9 +19,9 @@
     rows_buf, gain_buf, wq_buf, wkv_buf, q_stage, kv_stage,
     x_sem, gain_sem, load_sem,
     part_send, part_recv, link_send, link_recv, core_send, core_recv, side_send, side_recv, last_send, last_recv,
-    middle_send, middle_recv, ready_sem, pair_sem,
+    middle_send, middle_recv, ready_sem, pair_sem, lent_buf, lent_sem, early_sem,
     near_send, near_recv, far_send, far_recv, cross_send, cross_recv, pass_send, pass_recv,
-    *, norm_tile, dot_tile, shift,
+    *, norm_tile, dot_tile, shift, lent, early,
 ):
     n_rows, depth = rows_buf.shape
     heads = wq_hbm.shape[0]
@@ -50,7 +50,7 @@
         if depth_half is None:
             return wq_buf.at[slot, j - FIRST_HEAD]
         if j == last_head:
-            start = pl.multiple_of(depth_half * (half + shift), 16)
+            start = pl.multiple_of(depth_half * (half + shift), 8)
             return wq_buf.at[slot, j - FIRST_HEAD, pl.ds(start, half - shift)]
         return wq_buf.at[slot, j - FIRST_HEAD, pl.ds(pl.multiple_of(depth_half * half, half), half)]
 
@@ -112,6 +112,16 @@
         far.append(remote(q_stage.at[1, 0] if h == 0 else late_out.at[h - 1], q_out.at[h, my_rows], far_send.at[2 + h], far_recv.at[2 + h], across))
         cross.append(remote(q_stage.at[2, h], q_out.at[h, my_rows], cross_send.at[h], cross_recv.at[h], across_other))
 
+    last_h = heads - 1
+    lent_rows, kept_rows = pl.ds(0, lent), pl.ds(lent, n_rows - lent)
+    my_kept = pl.ds(pl.multiple_of(member * n_rows + lent, lent), n_rows - lent)
+    partner_lent = pl.ds(pl.multiple_of((chip * 2 + 1 - core) * n_rows, n_rows), lent)
+    lend = remote(q_stage.at[2, last_h, lent_rows], lent_buf, lent_sem.at[0], lent_sem.at[1], partner)
+    cross_kept = remote(q_stage.at[2, last_h, kept_rows], q_out.at[last_h, my_kept], cross_send.at[last_h], cross_recv.at[last_h], across_other)
+    cross_lent = remote(lent_buf, q_out.at[last_h, partner_lent], lent_sem.at[2], lent_sem.at[3], across)
+    my_early = pl.ds(pl.multiple_of(member * n_rows, n_rows), early)
+    early_far = remote(late_out.at[0, pl.ds(0, early)], q_out.at[1, my_early], early_sem.at[0], early_sem.at[1], across)
+
     firsts[0].wait()
     link[0].start()
     for load in head_loads[:1] + rests + head_loads[1:] + [gain_load] + x_loads:
@@ -176,6 +186,9 @@
 
     def own_rows_at(start):
         return pl.ds(pl.multiple_of(member * n_rows + start, dot_tile), dot_tile)
+
+    def when(condition, act):
+        pl.when(condition)(act)
 
     def own_q(h):
         def store(start, value):
@@ -275,11 +288,19 @@
     middle_hand.wait_recv()
     staged_q(2, 3, 2)
     late_q(2)
-    cross[2].start()
+    when(core == 0, lend.start)
     own_q(2)
 
+    @pl.when(core == 1)
+    def _():
+        lend.wait_recv()
+        cross_lent.start()
+        early_far.start()
+        cross[last_h].start()
+
     @pl.when(core == 0)
     def _():
+        cross_kept.start()
         for copy in far[FIRST_HEAD:]:
             copy.start()
 
@@ -302,7 +323,7 @@
         middle_link.wait_send()
         middle_side.wait_send()
 
-    for copy in near + passed + cross:
+    for copy in near + passed + cross[:last_h]:
         copy.wait()
     for copy in far[:FIRST_HEAD]:
         copy.wait_send()
@@ -312,9 +333,19 @@
     def _():
         for copy in far[FIRST_HEAD + 1:]:
             copy.wait()
-
-
-def finish_kernel(q_ref, k_ref, v_ref, q_out, k_out, v_out, sems):
+        lend.wait_send()
+        cross_kept.wait_send()
+        cross[last_h].wait_recv()
+
+    @pl.when(core == 1)
+    def _():
+        cross[last_h].wait_send()
+        early_far.wait()
+        cross_lent.wait()
+        cross_kept.wait_recv()
+
+
+def finish_kernel(q_ref, k_ref, v_ref, q_out, k_out, v_out, sems, *, early):
     member = lax.axis_index("tp")
     chip, core = member // 2, member % 2
     n_rows = q_ref.shape[1] // 4
@@ -329,6 +360,13 @@
     for copy in here:
         copy.start()
 
+    early_rows = pl.ds(pl.multiple_of((3 - 2 * chip) * n_rows, n_rows), early)
+    early_copy = pltpu.make_async_copy(q_ref.at[1, early_rows], q_out.at[1, early_rows], sems.at[len(here) + len(there)])
+
+    @pl.when(core == 1)
+    def _():
+        early_copy.start()
+
     @pl.when(core == 0)
     def _():
         for copy in there:
@@ -337,13 +375,21 @@
     for copy in here:
         copy.wait()
 
+    @pl.when(core == 1)
+    def _():
+        early_copy.wait()
+
     @pl.when(core == 0)
     def _():
         for copy in there:
             copy.wait()
 
 
-def late_kernel(after_ref, late_out, late_in, send_sem, recv_sem):
+def late_cut(early, n_rows, i):
+    return pl.ds(early, n_rows - early) if i == 0 else pl.ds(0, n_rows)
+
+
+def late_kernel(after_ref, late_out, late_in, send_sem, recv_sem, *, early):
     group, member = lax.axis_index("dp"), lax.axis_index("tp")
 
     @pl.when(member % 2 == 1)
@@ -353,9 +399,9 @@
         pl.semaphore_signal(barrier, inc=1, device_id=across, device_id_type=MESH)
         pl.semaphore_wait(barrier, 1)
         copies = [
-            pltpu.make_async_remote_copy(src_ref=late_out.at[i], dst_ref=late_in.at[i], send_sem=send_sem.at[i], recv_sem=recv_sem.at[i],
-                                         device_id=across, device_id_type=MESH)
-            for i in range(late_out.shape[0])
+            pltpu.make_async_remote_copy(src_ref=late_out.at[i, cut], dst_ref=late_in.at[i, cut], send_sem=send_sem.at[i],
+                                         recv_sem=recv_sem.at[i], device_id=across, device_id_type=MESH)
+            for i, cut in enumerate(late_cut(early, late_out.shape[1], i) for i in range(late_out.shape[0]))
         ]
         for copy in copies:
             copy.start()
@@ -363,14 +409,18 @@
             copy.wait()
 
 
-def patch_kernel(before_ref, late_ref, q_out, sems):
+def patch_kernel(before_ref, late_ref, q_out, sems, *, early):
     member = lax.axis_index("tp")
     n_rows = late_ref.shape[1]
 
     @pl.when(member % 2 == 1)
     def _():
-        where = pl.ds(pl.multiple_of(((member + 2) % 4) * n_rows, n_rows), n_rows)
-        copies = [pltpu.make_async_copy(late_ref.at[i], q_out.at[1 + i, where], sems.at[i]) for i in range(late_ref.shape[0])]
+        base = ((member + 2) % 4) * n_rows
+        copies = []
+        for i in range(late_ref.shape[0]):
+            cut = late_cut(early, n_rows, i)
+            where = pl.ds(pl.multiple_of(base + cut.start, early), cut.size)
+            copies.append(pltpu.make_async_copy(late_ref.at[i, cut], q_out.at[1 + i, where], sems.at[i]))
         for copy in copies:
             copy.start()
         for copy in copies:
@@ -387,12 +437,13 @@
         all_rows = members * n_rows
         dma = pltpu.SemaphoreType.DMA
         norm_tile = n_rows // 4
+        shift, lent, early = 72, 128, 512
         vmem = pl.BlockSpec(memory_space=pltpu.VMEM)
         results = tuple(jax.ShapeDtypeStruct((n, all_rows, width), jnp.bfloat16) for n in (heads, 1, 1))
         hbm = pl.BlockSpec(memory_space=pltpu.HBM)
         late_shape = jax.ShapeDtypeStruct((heads - 1, n_rows, width), jnp.bfloat16)
         q, k, v, late = pl.pallas_call(
-            functools.partial(qkv_kernel, norm_tile=norm_tile, dot_tile=256, shift=80),
+            functools.partial(qkv_kernel, norm_tile=norm_tile, dot_tile=256, shift=shift, lent=lent, early=early),
             out_shape=results + (late_shape,),
             in_specs=[hbm] * 5,
             out_specs=(vmem,) * 4,
@@ -406,6 +457,7 @@
                 dma((4,)), dma(()), dma((pieces + FIRST_HEAD,)),
                 *[dma((pieces,)) for _ in range(10)],
                 dma((3,)), dma((3,)), pltpu.SemaphoreType.REGULAR, pltpu.SemaphoreType.REGULAR,
+                pltpu.VMEM((lent, width), jnp.bfloat16), dma((4,)), dma((2,)),
                 dma((pieces,)), dma((pieces,)), dma((pieces,)), dma((pieces,)),
                 dma((heads,)), dma((heads,)), dma((2,)), dma((2,)),
             ],
@@ -414,16 +466,16 @@
             name="qkv",
         )(*[pltpu.with_memory_space_constraint(a, pltpu.HBM) for a in (x_rows, norm_gain, w_q.transpose(1, 0, 2), w_k.T, w_v.T)])
         q, k, v = pl.pallas_call(
-            finish_kernel,
+            functools.partial(finish_kernel, early=early),
             out_shape=results,
             in_specs=[vmem] * 3,
             out_specs=(hbm,) * 3,
-            scratch_shapes=[dma((4 * (heads + 2),))],
+            scratch_shapes=[dma((4 * (heads + 2) + 1,))],
             compiler_params=pltpu.CompilerParams(vmem_limit_bytes=16 * 1024 * 1024),
             name="finish",
         )(q, k, v)
         late = pl.pallas_call(
-            late_kernel,
+            functools.partial(late_kernel, early=early),
             out_shape=late_shape,
             in_specs=[hbm, vmem],
             out_specs=vmem,
@@ -432,7 +484,7 @@
             name="late",
         )(pltpu.with_memory_space_constraint(q, pltpu.HBM), late)
         q = pl.pallas_call(
-            patch_kernel,
+            functools.partial(patch_kernel, early=early),
             out_shape=results[0],
             in_specs=[hbm, vmem],
             out_specs=hbm,

time: 67.3 us -> 66.9 us (level)
    pallas_call x1, Pallas kernels: 52.4 us -> 56.1 us  [local_step(): pl.pallas_call(functools.partial(qkv_kernel, norm_tile=norm_tile, dot_til...]
    pallas_call x3, Pallas kernels: 13.7 us -> 10 us  [the longest x1 6.87 us: local_step(): pl.pallas_call(functools.partial(late_kernel, early=early), out_shape=lat...]
where the time goes in v10:
time: 66.9 us; the launch traced here: 66.8 us
  Pallas kernels  66.1 us (99%)
    pallas_call x1, Pallas kernels, local_step(): pl.pallas_call(functools.partial(qkv_kernel, norm_tile=norm_tile, dot_til...  56.1 us
    pallas_call x1, Pallas kernels, local_step(): pl.pallas_call(functools.partial(late_kernel, early=early), out_shape=lat...  6.87 us
    pallas_call x1, Pallas kernels, local_step(): pl.pallas_call(functools.partial(finish_kernel, early=early), out_shape=r...  2.4 us

profile of v10, /device:TPU:1, one launch (start us, length us, event | category | flops | bytes accessed | tf_op | source)
XLA Modules:
  0.0 66.8 jit_solution(3504572297541485904)
XLA Ops:
  0.6 56.1 %qkv.1 = (bf16[3,4096,128]{2,1,0:T(8,128)(2,1)S(1)}, bf16[1,4096,128]{2,1,0:T(8,128)(2,1)S(1)}, bf16[1,4096,128]{2,1,0:T(8,128)(2,1)S(1)}, bf16[2,1024,128]{2,1,0:T(8,128)(2,1)S(1)}) custom-call(bf16[1024,1536]{1,0:T(8,128)(2,1)} %x_hbm.1, f32[1536]{0:T(1024)} %gain_hbm.1, bf16[3,1536,128]{2,1,0:T(8,128)(2,1)} %bitcast.7, bf16[64,1536]{1,0:T(8,128)(2,1)} %bitcast.10, ...), custom_call_target="tpu_custom_call" | custom-call | flops 6442450944 | bytes 16777216 | tf_op jit(solution)/shard_map/qkv/pallas_call | solution.py:445
  56.7 2.4 %finish.1 = (bf16[3,4096,128]{2,1,0:T(8,128)(2,1)}, bf16[1,4096,128]{2,1,0:T(8,128)(2,1)}, bf16[1,4096,128]{2,1,0:T(8,128)(2,1)}) custom-call(bf16[3,4096,128]{2,1,0:T(8,128)(2,1)S(1)} %get-tuple-element.10.q_ref, bf16[1,4096,128]{2,1,0:T(8,128)(2,1)S(1)} %get-tuple-element.11.k_ref, bf16[1,4096,128]{2,1,0:T(8,128)(2,1)S(1)} %get-tuple-element.12.v_ref), custom_call_target="tpu_custom_call" | custom-call | tf_op jit(solution)/shard_map/finish/pallas_call | solution.py:468
  59.1 6.9 %late.1.late_ref = bf16[2,1024,128]{2,1,0:T(8,128)(2,1)S(1)} custom-call(bf16[3,4096,128]{2,1,0:T(8,128)(2,1)} %get-tuple-element.13.after_ref.before_ref, bf16[2,1024,128]{2,1,0:T(8,128)(2,1)S(1)} %get-tuple-element.14.late_out), custom_call_target="tpu_custom_call" | custom-call | tf_op jit(solution)/shard_map/late/pallas_call | solution.py:477
  66.0 0.8 %patch.1 = bf16[3,4096,128]{2,1,0:T(8,128)(2,1)} custom-call(bf16[3,4096,128]{2,1,0:T(8,128)(2,1)} %get-tuple-element.13.after_ref.before_ref, bf16[2,1024,128]{2,1,0:T(8,128)(2,1)S(1)} %late.1.late_ref), custom_call_target="tpu_custom_call", output_to_operand_aliasing={{}: (0, {})} | custom-call | tf_op jit(solution)/shard_map/patch/pallas_call | solution.py:486

commit v11 on v10

--- a/solution.py
+++ b/solution.py
@@ -77,6 +77,8 @@
         pltpu.make_async_copy(x_hbm.at[pl.ds(i * norm_tile, norm_tile)], rows_buf.at[pl.ds(i * norm_tile, norm_tile)], x_sem.at[i])
         for i in range(n_tiles)
     ]
+    for load in head_loads[:1] + rests + head_loads[1:] + [gain_load] + x_loads:
+        load.start()
     pl.semaphore_wait(barrier, 2 + group)
 
     def remote(src, dst, send, recv, device):
@@ -124,8 +126,6 @@
 
     firsts[0].wait()
     link[0].start()
-    for load in head_loads[:1] + rests + head_loads[1:] + [gain_load] + x_loads:
-        load.start()
     firsts[1].wait()
     link[1].start()
     for j in range(FIRST_HEAD, pieces):

time: 66.9 us -> 66.9 us (level)
  no operation moved by 1% of the time
where the time goes in v11:
time: 66.9 us; the launch traced here: 66.8 us
  Pallas kernels  66.1 us (99%)
    pallas_call x1, Pallas kernels, local_step(): pl.pallas_call(functools.partial(qkv_kernel, norm_tile=norm_tile, dot_til...  56.1 us
    pallas_call x1, Pallas kernels, local_step(): pl.pallas_call(functools.partial(late_kernel, early=early), out_shape=lat...  6.87 us
    pallas_call x1, Pallas kernels, local_step(): pl.pallas_call(functools.partial(finish_kernel, early=early), out_shape=r...  2.4 us

profile of v11, /device:TPU:1, one launch (start us, length us, event | category | flops | bytes accessed | tf_op | source)
XLA Modules:
  0.0 66.8 jit_solution(12216863936566726808)
XLA Ops:
  0.6 56.1 %qkv.1 = (bf16[3,4096,128]{2,1,0:T(8,128)(2,1)S(1)}, bf16[1,4096,128]{2,1,0:T(8,128)(2,1)S(1)}, bf16[1,4096,128]{2,1,0:T(8,128)(2,1)S(1)}, bf16[2,1024,128]{2,1,0:T(8,128)(2,1)S(1)}) custom-call(bf16[1024,1536]{1,0:T(8,128)(2,1)} %x_hbm.1, f32[1536]{0:T(1024)} %gain_hbm.1, bf16[3,1536,128]{2,1,0:T(8,128)(2,1)} %bitcast.7, bf16[64,1536]{1,0:T(8,128)(2,1)} %bitcast.10, ...), custom_call_target="tpu_custom_call" | custom-call | flops 6442450944 | bytes 16777216 | tf_op jit(solution)/shard_map/qkv/pallas_call | solution.py:445
  56.7 2.4 %finish.1 = (bf16[3,4096,128]{2,1,0:T(8,128)(2,1)}, bf16[1,4096,128]{2,1,0:T(8,128)(2,1)}, bf16[1,4096,128]{2,1,0:T(8,128)(2,1)}) custom-call(bf16[3,4096,128]{2,1,0:T(8,128)(2,1)S(1)} %get-tuple-element.10.q_ref, bf16[1,4096,128]{2,1,0:T(8,128)(2,1)S(1)} %get-tuple-element.11.k_ref, bf16[1,4096,128]{2,1,0:T(8,128)(2,1)S(1)} %get-tuple-element.12.v_ref), custom_call_target="tpu_custom_call" | custom-call | tf_op jit(solution)/shard_map/finish/pallas_call | solution.py:468
  59.1 6.9 %late.1.late_ref = bf16[2,1024,128]{2,1,0:T(8,128)(2,1)S(1)} custom-call(bf16[3,4096,128]{2,1,0:T(8,128)(2,1)} %get-tuple-element.13.after_ref.before_ref, bf16[2,1024,128]{2,1,0:T(8,128)(2,1)S(1)} %get-tuple-element.14.late_out), custom_call_target="tpu_custom_call" | custom-call | tf_op jit(solution)/shard_map/late/pallas_call | solution.py:477
  66.0 0.8 %patch.1 = bf16[3,4096,128]{2,1,0:T(8,128)(2,1)} custom-call(bf16[3,4096,128]{2,1,0:T(8,128)(2,1)} %get-tuple-element.13.after_ref.before_ref, bf16[2,1024,128]{2,1,0:T(8,128)(2,1)S(1)} %late.1.late_ref), custom_call_target="tpu_custom_call", output_to_operand_aliasing={{}: (0, {})} | custom-call | tf_op jit(solution)/shard_map/patch/pallas_call | solution.py:486

commit v12 on v11

--- a/solution.py
+++ b/solution.py
@@ -128,27 +128,28 @@
     link[0].start()
     firsts[1].wait()
     link[1].start()
+    pl.semaphore_signal(pair_sem, inc=1, device_id=across, device_id_type=MESH)
+
+    @pl.when(group == 1)
+    def _():
+        pl.semaphore_signal(ready_sem, inc=1, device_id=beside, device_id_type=MESH)
+
+    pl.semaphore_wait(pair_sem, 1)
     for j in range(FIRST_HEAD, pieces):
         head_loads[j - FIRST_HEAD].wait()
         link[j].start()
     for load in rests:
         load.wait()
-    pl.semaphore_signal(pair_sem, inc=1, device_id=across, device_id_type=MESH)
 
     @pl.when(group == 1)
     def _():
         middle_link.start()
-        pl.semaphore_signal(ready_sem, inc=1, device_id=beside, device_id_type=MESH)
 
     for copy in part:
         copy.start()
 
-    gain_load.wait()
     chunks = depth // LANES
     sub = 64
-
-    for i in range(n_tiles):
-        x_loads[i].wait()
 
     def norm_step(s, carry):
         here = pl.ds(pl.multiple_of(s * sub, sub), sub)
@@ -163,7 +164,11 @@
             rows_buf[here, cols] = (wide * scale * gain_buf[cols][None, :]).astype(jnp.bfloat16)
         return carry
 
-    lax.fori_loop(0, n_rows // sub, norm_step, 0)
+    def normalize():
+        gain_load.wait()
+        for load in x_loads:
+            load.wait()
+        lax.fori_loop(0, n_rows // sub, norm_step, 0)
 
     def over_tiles(step):
         lax.fori_loop(0, n_rows // dot_tile, lambda i, carry: (step(i * dot_tile), carry)[1], 0)
@@ -242,13 +247,12 @@
         hand[j].wait_recv()
         last[j].wait_recv()
 
-    pl.semaphore_wait(pair_sem, 1)
-
     @pl.when(group == 0)
     def _():
         pl.semaphore_wait(ready_sem, 1)
 
     from_link(K_PIECE)
+    normalize()
     from_link(V_PIECE)
     part[K_PIECE].wait_recv()
     part[V_PIECE].wait_recv()

time: 66.9 us -> 66.9 us (level)
  no operation moved by 1% of the time
where the time goes in v12:
time: 66.9 us; the launch traced here: 66.8 us
  Pallas kernels  66.1 us (99%)
    pallas_call x1, Pallas kernels, local_step(): pl.pallas_call(functools.partial(qkv_kernel, norm_tile=norm_tile, dot_til...  56.1 us
    pallas_call x1, Pallas kernels, local_step(): pl.pallas_call(functools.partial(late_kernel, early=early), out_shape=lat...  6.87 us
    pallas_call x1, Pallas kernels, local_step(): pl.pallas_call(functools.partial(finish_kernel, early=early), out_shape=r...  2.4 us

profile of v12, /device:TPU:1, one launch (start us, length us, event | category | flops | bytes accessed | tf_op | source)
XLA Modules:
  0.0 66.8 jit_solution(7146060317217906840)
XLA Ops:
  0.6 56.1 %qkv.1 = (bf16[3,4096,128]{2,1,0:T(8,128)(2,1)S(1)}, bf16[1,4096,128]{2,1,0:T(8,128)(2,1)S(1)}, bf16[1,4096,128]{2,1,0:T(8,128)(2,1)S(1)}, bf16[2,1024,128]{2,1,0:T(8,128)(2,1)S(1)}) custom-call(bf16[1024,1536]{1,0:T(8,128)(2,1)} %x_hbm.1, f32[1536]{0:T(1024)} %gain_hbm.1, bf16[3,1536,128]{2,1,0:T(8,128)(2,1)} %bitcast.7, bf16[64,1536]{1,0:T(8,128)(2,1)} %bitcast.10, ...), custom_call_target="tpu_custom_call" | custom-call | flops 6442450944 | bytes 16777216 | tf_op jit(solution)/shard_map/qkv/pallas_call | solution.py:449
  56.7 2.4 %finish.1 = (bf16[3,4096,128]{2,1,0:T(8,128)(2,1)}, bf16[1,4096,128]{2,1,0:T(8,128)(2,1)}, bf16[1,4096,128]{2,1,0:T(8,128)(2,1)}) custom-call(bf16[3,4096,128]{2,1,0:T(8,128)(2,1)S(1)} %get-tuple-element.10.q_ref, bf16[1,4096,128]{2,1,0:T(8,128)(2,1)S(1)} %get-tuple-element.11.k_ref, bf16[1,4096,128]{2,1,0:T(8,128)(2,1)S(1)} %get-tuple-element.12.v_ref), custom_call_target="tpu_custom_call" | custom-call | tf_op jit(solution)/shard_map/finish/pallas_call | solution.py:472
  59.1 6.9 %late.1.late_ref = bf16[2,1024,128]{2,1,0:T(8,128)(2,1)S(1)} custom-call(bf16[3,4096,128]{2,1,0:T(8,128)(2,1)} %get-tuple-element.13.after_ref.before_ref, bf16[2,1024,128]{2,1,0:T(8,128)(2,1)S(1)} %get-tuple-element.14.late_out), custom_call_target="tpu_custom_call" | custom-call | tf_op jit(solution)/shard_map/late/pallas_call | solution.py:481
  66.0 0.8 %patch.1 = bf16[3,4096,128]{2,1,0:T(8,128)(2,1)} custom-call(bf16[3,4096,128]{2,1,0:T(8,128)(2,1)} %get-tuple-element.13.after_ref.before_ref, bf16[2,1024,128]{2,1,0:T(8,128)(2,1)S(1)} %late.1.late_ref), custom_call_target="tpu_custom_call", output_to_operand_aliasing={{}: (0, {})} | custom-call | tf_op jit(solution)/shard_map/patch/pallas_call | solution.py:490

commit v13 on v12

--- a/solution.py
+++ b/solution.py
@@ -19,7 +19,7 @@
     rows_buf, gain_buf, wq_buf, wkv_buf, q_stage, kv_stage,
     x_sem, gain_sem, load_sem,
     part_send, part_recv, link_send, link_recv, core_send, core_recv, side_send, side_recv, last_send, last_recv,
-    middle_send, middle_recv, ready_sem, pair_sem, lent_buf, lent_sem, early_sem,
+    middle_send, middle_recv, ready_sem, pair_sem, mate_sem, lent_buf, lent_sem, early_sem,
     near_send, near_recv, far_send, far_recv, cross_send, cross_recv, pass_send, pass_recv,
     *, norm_tile, dot_tile, shift, lent, early,
 ):
@@ -54,32 +54,26 @@
             return wq_buf.at[slot, j - FIRST_HEAD, pl.ds(start, half - shift)]
         return wq_buf.at[slot, j - FIRST_HEAD, pl.ds(pl.multiple_of(depth_half * half, half), half)]
 
-    firsts, rests = [], []
-    for j in range(FIRST_HEAD):
-        for copies, which, sem in ((firsts, group, j), (rests, 1 - group, pieces + j)):
-            cols = pl.ds(pl.multiple_of(which * half, half), half)
-            copies.append(pltpu.make_async_copy(sources[j].at[:, cols], piece_at(j, 0, which), load_sem.at[sem]))
-    head_loads = [pltpu.make_async_copy(sources[j], piece_at(j, 0), load_sem.at[j]) for j in range(FIRST_HEAD, pieces)]
-    for load in firsts:
-        load.start()
-
     barrier = pltpu.get_barrier_semaphore()
-    for other in (across, partner):
-        pl.semaphore_signal(barrier, inc=1, device_id=other, device_id_type=MESH)
-
-    @pl.when(group == 0)
-    def _():
-        pl.semaphore_signal(barrier, inc=1, device_id=beside, device_id_type=MESH)
-
+
+    def signal(sem, device):
+        pl.semaphore_signal(sem, inc=1, device_id=device, device_id_type=MESH)
+
+    def when(condition, act):
+        pl.when(condition)(act)
+
+    signal(barrier, across)
+    when(core == 1, lambda: signal(barrier, partner))
+    when(group == 0, lambda: signal(barrier, beside))
+    pl.semaphore_wait(barrier, 2 + group - core)
+
+    loads = [pltpu.make_async_copy(sources[j], piece_at(j, 0), load_sem.at[j]) for j in range(pieces)]
     gain_load = pltpu.make_async_copy(gain_hbm, gain_buf, gain_sem)
     n_tiles = n_rows // norm_tile
     x_loads = [
         pltpu.make_async_copy(x_hbm.at[pl.ds(i * norm_tile, norm_tile)], rows_buf.at[pl.ds(i * norm_tile, norm_tile)], x_sem.at[i])
         for i in range(n_tiles)
     ]
-    for load in head_loads[:1] + rests + head_loads[1:] + [gain_load] + x_loads:
-        load.start()
-    pl.semaphore_wait(barrier, 2 + group)
 
     def remote(src, dst, send, recv, device):
         return pltpu.make_async_remote_copy(src_ref=src, dst_ref=dst, send_sem=send, recv_sem=recv, device_id=device, device_id_type=MESH)
@@ -87,18 +81,28 @@
     part, link, hand, side, last = [], [], [], [], []
     for j in range(pieces):
         part.append(remote(piece_at(j, 0), piece_at(j, 0 if j < FIRST_HEAD else 1), part_send.at[j], part_recv.at[j], partner))
-        link.append(remote(piece_at(j, 0, group), piece_at(j, 2, group), link_send.at[j], link_recv.at[j], across))
+        sent = sources[j].at[:, pl.ds(pl.multiple_of(group * half, half), half)] if j < FIRST_HEAD else piece_at(j, 0, group)
+        link.append(remote(sent, piece_at(j, 2, group), link_send.at[j], link_recv.at[j], across))
         arrived, other_half = piece_at(j, 2, group), piece_at(j, 2, 1 - group)
         hand.append(remote(arrived, piece_at(j, 2 if j < FIRST_HEAD else 3, group), core_send.at[j], core_recv.at[j], partner))
         side.append(remote(arrived, arrived, side_send.at[j], side_recv.at[j], beside))
         last.append(remote(other_half, piece_at(j, 2 if j < FIRST_HEAD else 3, 1 - group), last_send.at[j], last_recv.at[j], partner))
 
-    def middle_at(slot):
-        return wq_buf.at[slot, heads - 1, middle]
-
-    middle_link = remote(middle_at(0), middle_at(2), middle_send.at[0], middle_recv.at[0], across)
-    middle_side = remote(middle_at(2), middle_at(2), middle_send.at[1], middle_recv.at[1], beside)
-    middle_hand = remote(middle_at(2), middle_at(3), middle_send.at[2], middle_recv.at[2], partner)
+    def middle_at(slot, part_of=None):
+        if part_of is None:
+            return wq_buf.at[slot, heads - 1, middle]
+        return wq_buf.at[slot, heads - 1, pl.ds(pl.multiple_of(half - shift + part_of * shift, 8), shift)]
+
+    def middle_copy(i, source_slot, slot, device, part_of=None):
+        return remote(middle_at(source_slot, part_of), middle_at(slot, part_of), middle_send.at[i], middle_recv.at[i], device)
+
+    middle_link = middle_copy(0, 0, 2, across)
+    middle_side = middle_copy(1, 2, 2, beside)
+    middle_hand = middle_copy(2, 2, 3, partner)
+    half_link = middle_copy(3, 0, 2, across, group)
+    half_side = middle_copy(4, 2, 2, beside, group)
+    half_hand = middle_copy(5, 2, 3, partner, group)
+    half_last = middle_copy(6, 2, 3, partner, 1 - group)
 
     my_rows = pl.ds(pl.multiple_of(member * n_rows, n_rows), n_rows)
     across_rows = pl.ds(pl.multiple_of(((1 - chip) * 2 + core) * n_rows, n_rows), n_rows)
@@ -124,27 +128,22 @@
     my_early = pl.ds(pl.multiple_of(member * n_rows, n_rows), early)
     early_far = remote(late_out.at[0, pl.ds(0, early)], q_out.at[1, my_early], early_sem.at[0], early_sem.at[1], across)
 
-    firsts[0].wait()
-    link[0].start()
-    firsts[1].wait()
-    link[1].start()
-    pl.semaphore_signal(pair_sem, inc=1, device_id=across, device_id_type=MESH)
-
-    @pl.when(group == 1)
-    def _():
-        pl.semaphore_signal(ready_sem, inc=1, device_id=beside, device_id_type=MESH)
-
+    for j in range(FIRST_HEAD):
+        link[j].start()
+    for load in loads + [gain_load] + x_loads:
+        load.start()
+
+    when(core == 0, lambda: signal(mate_sem, partner))
+    when(core == 1, lambda: pl.semaphore_wait(mate_sem, 1))
+    signal(pair_sem, across)
+    when(group == 1, lambda: signal(ready_sem, beside))
     pl.semaphore_wait(pair_sem, 1)
-    for j in range(FIRST_HEAD, pieces):
-        head_loads[j - FIRST_HEAD].wait()
-        link[j].start()
-    for load in rests:
-        load.wait()
-
-    @pl.when(group == 1)
-    def _():
-        middle_link.start()
-
+    for j in range(pieces):
+        loads[j].wait()
+        if j >= FIRST_HEAD:
+            link[j].start()
+    when(chip == 0, half_link.start)
+    when((chip == 1) & (group == 1), middle_link.start)
     for copy in part:
         copy.start()
 
@@ -192,9 +191,6 @@
     def own_rows_at(start):
         return pl.ds(pl.multiple_of(member * n_rows + start, dot_tile), dot_tile)
 
-    def when(condition, act):
-        pl.when(condition)(act)
-
     def own_q(h):
         def store(start, value):
             q_out[h, own_rows_at(start), :] = value
@@ -232,16 +228,31 @@
         last[j].start()
 
     def from_middle():
-        @pl.when(group == 1)
+        @pl.when(chip == 0)
         def _():
-            middle_link.wait_recv()
-            middle_side.start()
-
-        @pl.when(group == 0)
+            @pl.when(group == 1)
+            def _():
+                middle_link.wait_recv()
+                middle_side.start()
+
+            when(group == 0, middle_side.wait_recv)
+            middle_hand.start()
+
+        @pl.when(chip == 1)
         def _():
-            middle_side.wait_recv()
-
-        middle_hand.start()
+            half_link.wait_recv()
+            half_side.start()
+            half_hand.start()
+            half_side.wait_recv()
+            half_last.start()
+
+    def complete_middle():
+        when(chip == 0, middle_hand.wait_recv)
+
+        @pl.when(chip == 1)
+        def _():
+            half_hand.wait_recv()
+            half_last.wait_recv()
 
     def complete(j):
         hand[j].wait_recv()
@@ -289,7 +300,7 @@
     from_middle()
     cross[1].start()
     complete(4)
-    middle_hand.wait_recv()
+    complete_middle()
     staged_q(2, 3, 2)
     late_q(2)
     when(core == 0, lend.start)
@@ -319,13 +330,20 @@
     passed[1].start()
     near[2 + heads - 1].start()
 
-    for copy in part + link + hand + side + last + [middle_hand]:
+    for copy in part + link + hand + side + last:
         copy.wait_send()
 
-    @pl.when(group == 1)
-    def _():
-        middle_link.wait_send()
-        middle_side.wait_send()
+    @pl.when(chip == 0)
+    def _():
+        half_link.wait_send()
+        middle_hand.wait_send()
+        when(group == 1, middle_side.wait_send)
+
+    @pl.when(chip == 1)
+    def _():
+        when(group == 1, middle_link.wait_send)
+        for copy in (half_side, half_hand, half_last):
+            copy.wait_send()
 
     for copy in near + passed + cross[:last_h]:
         copy.wait()
@@ -441,7 +459,7 @@
         all_rows = members * n_rows
         dma = pltpu.SemaphoreType.DMA
         norm_tile = n_rows // 4
-        shift, lent, early = 72, 128, 512
+        shift, lent, early = 56, 128, 512
         vmem = pl.BlockSpec(memory_space=pltpu.VMEM)
         results = tuple(jax.ShapeDtypeStruct((n, all_rows, width), jnp.bfloat16) for n in (heads, 1, 1))
         hbm = pl.BlockSpec(memory_space=pltpu.HBM)
@@ -458,9 +476,9 @@
                 pltpu.VMEM((2, 4 * share, depth), jnp.bfloat16),
                 pltpu.VMEM((3, heads, n_rows, width), jnp.bfloat16),
                 pltpu.VMEM((2, n_rows, width), jnp.bfloat16),
-                dma((4,)), dma(()), dma((pieces + FIRST_HEAD,)),
+                dma((4,)), dma(()), dma((pieces,)),
                 *[dma((pieces,)) for _ in range(10)],
-                dma((3,)), dma((3,)), pltpu.SemaphoreType.REGULAR, pltpu.SemaphoreType.REGULAR,
+                dma((7,)), dma((7,)), pltpu.SemaphoreType.REGULAR, pltpu.SemaphoreType.REGULAR, pltpu.SemaphoreType.REGULAR,
                 pltpu.VMEM((lent, width), jnp.bfloat16), dma((4,)), dma((2,)),
                 dma((pieces,)), dma((pieces,)), dma((pieces,)), dma((pieces,)),
                 dma((heads,)), dma((heads,)), dma((2,)), dma((2,)),

time: 66.9 us -> 67.1 us (level)
  no operation moved by 1% of the time
where the time goes in v13:
time: 67.1 us; the launch traced here: 67 us
  Pallas kernels  66.4 us (99%)
    pallas_call x1, Pallas kernels, local_step(): pl.pallas_call(functools.partial(qkv_kernel, norm_tile=norm_tile, dot_til...  56.5 us
    pallas_call x1, Pallas kernels, local_step(): pl.pallas_call(functools.partial(late_kernel, early=early), out_shape=lat...  6.68 us
    pallas_call x1, Pallas kernels, local_step(): pl.pallas_call(functools.partial(finish_kernel, early=early), out_shape=r...  2.4 us

profile of v13, /device:TPU:1, one launch (start us, length us, event | category | flops | bytes accessed | tf_op | source)
XLA Modules:
  0.0 67.0 jit_solution(1343546163546121353)
XLA Ops:
  0.6 56.5 %qkv.1 = (bf16[3,4096,128]{2,1,0:T(8,128)(2,1)S(1)}, bf16[1,4096,128]{2,1,0:T(8,128)(2,1)S(1)}, bf16[1,4096,128]{2,1,0:T(8,128)(2,1)S(1)}, bf16[2,1024,128]{2,1,0:T(8,128)(2,1)S(1)}) custom-call(bf16[1024,1536]{1,0:T(8,128)(2,1)} %x_hbm.1, f32[1536]{0:T(1024)} %gain_hbm.1, bf16[3,1536,128]{2,1,0:T(8,128)(2,1)} %bitcast.7, bf16[64,1536]{1,0:T(8,128)(2,1)} %bitcast.10, ...), custom_call_target="tpu_custom_call" | custom-call | flops 6442450944 | bytes 16777216 | tf_op jit(solution)/shard_map/qkv/pallas_call | solution.py:467
  57.1 2.4 %finish.1 = (bf16[3,4096,128]{2,1,0:T(8,128)(2,1)}, bf16[1,4096,128]{2,1,0:T(8,128)(2,1)}, bf16[1,4096,128]{2,1,0:T(8,128)(2,1)}) custom-call(bf16[3,4096,128]{2,1,0:T(8,128)(2,1)S(1)} %get-tuple-element.10.q_ref, bf16[1,4096,128]{2,1,0:T(8,128)(2,1)S(1)} %get-tuple-element.11.k_ref, bf16[1,4096,128]{2,1,0:T(8,128)(2,1)S(1)} %get-tuple-element.12.v_ref), custom_call_target="tpu_custom_call" | custom-call | tf_op jit(solution)/shard_map/finish/pallas_call | solution.py:490
  59.5 6.7 %late.1.late_ref = bf16[2,1024,128]{2,1,0:T(8,128)(2,1)S(1)} custom-call(bf16[3,4096,128]{2,1,0:T(8,128)(2,1)} %get-tuple-element.13.after_ref.before_ref, bf16[2,1024,128]{2,1,0:T(8,128)(2,1)S(1)} %get-tuple-element.14.late_out), custom_call_target="tpu_custom_call" | custom-call | tf_op jit(solution)/shard_map/late/pallas_call | solution.py:499
  66.2 0.8 %patch.1 = bf16[3,4096,128]{2,1,0:T(8,128)(2,1)} custom-call(bf16[3,4096,128]{2,1,0:T(8,128)(2,1)} %get-tuple-element.13.after_ref.before_ref, bf16[2,1024,128]{2,1,0:T(8,128)(2,1)S(1)} %late.1.late_ref), custom_call_target="tpu_custom_call", output_to_operand_aliasing={{}: (0, {})} | custom-call | tf_op jit(solution)/shard_map/patch/pallas_call | solution.py:508

commit v14 on v13

--- a/solution.py
+++ b/solution.py
@@ -459,7 +459,7 @@
         all_rows = members * n_rows
         dma = pltpu.SemaphoreType.DMA
         norm_tile = n_rows // 4
-        shift, lent, early = 56, 128, 512
+        shift, lent, early = 56, 128, 256
         vmem = pl.BlockSpec(memory_space=pltpu.VMEM)
         results = tuple(jax.ShapeDtypeStruct((n, all_rows, width), jnp.bfloat16) for n in (heads, 1, 1))
         hbm = pl.BlockSpec(memory_space=pltpu.HBM)

time: 67.1 us -> 66.4 us (0.990)
  Pallas kernels: 66.4 us -> 65.7 us
    pallas_call x1, Pallas kernels: 56.5 us -> 55.1 us  [local_step(): pl.pallas_call(functools.partial(qkv_kernel, norm_tile=norm_tile, dot_til...]
    pallas_call x1, Pallas kernels: 6.68 us -> 7.39 us  [local_step(): pl.pallas_call(functools.partial(late_kernel, early=early), out_shape=lat...]
where the time goes in v14:
time: 66.4 us; the launch traced here: 66.3 us
  Pallas kernels  65.7 us (99%)
    pallas_call x1, Pallas kernels, local_step(): pl.pallas_call(functools.partial(qkv_kernel, norm_tile=norm_tile, dot_til...  55.1 us
    pallas_call x1, Pallas kernels, local_step(): pl.pallas_call(functools.partial(late_kernel, early=early), out_shape=lat...  7.39 us
    pallas_call x1, Pallas kernels, local_step(): pl.pallas_call(functools.partial(finish_kernel, early=early), out_shape=r...  2.37 us

profile of v14, /device:TPU:1, one launch (start us, length us, event | category | flops | bytes accessed | tf_op | source)
XLA Modules:
  0.0 66.3 jit_solution(10547669642666798859)
XLA Ops:
  0.6 55.1 %qkv.1 = (bf16[3,4096,128]{2,1,0:T(8,128)(2,1)S(1)}, bf16[1,4096,128]{2,1,0:T(8,128)(2,1)S(1)}, bf16[1,4096,128]{2,1,0:T(8,128)(2,1)S(1)}, bf16[2,1024,128]{2,1,0:T(8,128)(2,1)S(1)}) custom-call(bf16[1024,1536]{1,0:T(8,128)(2,1)} %x_hbm.1, f32[1536]{0:T(1024)} %gain_hbm.1, bf16[3,1536,128]{2,1,0:T(8,128)(2,1)} %bitcast.7, bf16[64,1536]{1,0:T(8,128)(2,1)} %bitcast.10, ...), custom_call_target="tpu_custom_call" | custom-call | flops 6442450944 | bytes 16777216 | tf_op jit(solution)/shard_map/qkv/pallas_call | solution.py:467
  55.7 2.4 %finish.1 = (bf16[3,4096,128]{2,1,0:T(8,128)(2,1)}, bf16[1,4096,128]{2,1,0:T(8,128)(2,1)}, bf16[1,4096,128]{2,1,0:T(8,128)(2,1)}) custom-call(bf16[3,4096,128]{2,1,0:T(8,128)(2,1)S(1)} %get-tuple-element.10.q_ref, bf16[1,4096,128]{2,1,0:T(8,128)(2,1)S(1)} %get-tuple-element.11.k_ref, bf16[1,4096,128]{2,1,0:T(8,128)(2,1)S(1)} %get-tuple-element.12.v_ref), custom_call_target="tpu_custom_call" | custom-call | tf_op jit(solution)/shard_map/finish/pallas_call | solution.py:490
  58.1 7.4 %late.1.late_ref = bf16[2,1024,128]{2,1,0:T(8,128)(2,1)S(1)} custom-call(bf16[3,4096,128]{2,1,0:T(8,128)(2,1)} %get-tuple-element.13.after_ref.before_ref, bf16[2,1024,128]{2,1,0:T(8,128)(2,1)S(1)} %get-tuple-element.14.late_out), custom_call_target="tpu_custom_call" | custom-call | tf_op jit(solution)/shard_map/late/pallas_call | solution.py:499
  65.5 0.8 %patch.1 = bf16[3,4096,128]{2,1,0:T(8,128)(2,1)} custom-call(bf16[3,4096,128]{2,1,0:T(8,128)(2,1)} %get-tuple-element.13.after_ref.before_ref, bf16[2,1024,128]{2,1,0:T(8,128)(2,1)S(1)} %late.1.late_ref), custom_call_target="tpu_custom_call", output_to_operand_aliasing={{}: (0, {})} | custom-call | tf_op jit(solution)/shard_map/patch/pallas_call | solution.py:508

commit v15 on v14

--- a/solution.py
+++ b/solution.py
@@ -459,7 +459,7 @@
         all_rows = members * n_rows
         dma = pltpu.SemaphoreType.DMA
         norm_tile = n_rows // 4
-        shift, lent, early = 56, 128, 256
+        shift, lent, early = 56, 128, 128
         vmem = pl.BlockSpec(memory_space=pltpu.VMEM)
         results = tuple(jax.ShapeDtypeStruct((n, all_rows, width), jnp.bfloat16) for n in (heads, 1, 1))
         hbm = pl.BlockSpec(memory_space=pltpu.HBM)

time: 66.4 us -> 66.1 us (level)
    pallas_call x1, Pallas kernels: 55.1 us -> 54.4 us  [local_step(): pl.pallas_call(functools.partial(qkv_kernel, norm_tile=norm_tile, dot_til...]
where the time goes in v15:
time: 66.1 us; the launch traced here: 66 us
  Pallas kernels  65.4 us (99%)
    pallas_call x1, Pallas kernels, local_step(): pl.pallas_call(functools.partial(qkv_kernel, norm_tile=norm_tile, dot_til...  54.4 us
    pallas_call x1, Pallas kernels, local_step(): pl.pallas_call(functools.partial(late_kernel, early=early), out_shape=lat...  7.78 us
    pallas_call x1, Pallas kernels, local_step(): pl.pallas_call(functools.partial(finish_kernel, early=early), out_shape=r...  2.37 us

profile of v15, /device:TPU:1, one launch (start us, length us, event | category | flops | bytes accessed | tf_op | source)
XLA Modules:
  0.0 66.0 jit_solution(10978493744951650724)
XLA Ops:
  0.6 54.4 %qkv.1 = (bf16[3,4096,128]{2,1,0:T(8,128)(2,1)S(1)}, bf16[1,4096,128]{2,1,0:T(8,128)(2,1)S(1)}, bf16[1,4096,128]{2,1,0:T(8,128)(2,1)S(1)}, bf16[2,1024,128]{2,1,0:T(8,128)(2,1)S(1)}) custom-call(bf16[1024,1536]{1,0:T(8,128)(2,1)} %x_hbm.1, f32[1536]{0:T(1024)} %gain_hbm.1, bf16[3,1536,128]{2,1,0:T(8,128)(2,1)} %bitcast.7, bf16[64,1536]{1,0:T(8,128)(2,1)} %bitcast.10, ...), custom_call_target="tpu_custom_call" | custom-call | flops 6442450944 | bytes 16777216 | tf_op jit(solution)/shard_map/qkv/pallas_call | solution.py:467
  55.0 2.4 %finish.1 = (bf16[3,4096,128]{2,1,0:T(8,128)(2,1)}, bf16[1,4096,128]{2,1,0:T(8,128)(2,1)}, bf16[1,4096,128]{2,1,0:T(8,128)(2,1)}) custom-call(bf16[3,4096,128]{2,1,0:T(8,128)(2,1)S(1)} %get-tuple-element.10.q_ref, bf16[1,4096,128]{2,1,0:T(8,128)(2,1)S(1)} %get-tuple-element.11.k_ref, bf16[1,4096,128]{2,1,0:T(8,128)(2,1)S(1)} %get-tuple-element.12.v_ref), custom_call_target="tpu_custom_call" | custom-call | tf_op jit(solution)/shard_map/finish/pallas_call | solution.py:490
  57.4 7.8 %late.1.late_ref = bf16[2,1024,128]{2,1,0:T(8,128)(2,1)S(1)} custom-call(bf16[3,4096,128]{2,1,0:T(8,128)(2,1)} %get-tuple-element.13.after_ref.before_ref, bf16[2,1024,128]{2,1,0:T(8,128)(2,1)S(1)} %get-tuple-element.14.late_out), custom_call_target="tpu_custom_call" | custom-call | tf_op jit(solution)/shard_map/late/pallas_call | solution.py:499
  65.2 0.8 %patch.1 = bf16[3,4096,128]{2,1,0:T(8,128)(2,1)} custom-call(bf16[3,4096,128]{2,1,0:T(8,128)(2,1)} %get-tuple-element.13.after_ref.before_ref, bf16[2,1024,128]{2,1,0:T(8,128)(2,1)S(1)} %late.1.late_ref), custom_call_target="tpu_custom_call", output_to_operand_aliasing={{}: (0, {})} | custom-call | tf_op jit(solution)/shard_map/patch/pallas_call | solution.py:508

commit v16 on v15

--- a/solution.py
+++ b/solution.py
@@ -120,13 +120,13 @@
 
     last_h = heads - 1
     lent_rows, kept_rows = pl.ds(0, lent), pl.ds(lent, n_rows - lent)
-    my_kept = pl.ds(pl.multiple_of(member * n_rows + lent, lent), n_rows - lent)
+    my_kept = pl.ds(pl.multiple_of(member * n_rows + lent, LANES), n_rows - lent)
     partner_lent = pl.ds(pl.multiple_of((chip * 2 + 1 - core) * n_rows, n_rows), lent)
     lend = remote(q_stage.at[2, last_h, lent_rows], lent_buf, lent_sem.at[0], lent_sem.at[1], partner)
     cross_kept = remote(q_stage.at[2, last_h, kept_rows], q_out.at[last_h, my_kept], cross_send.at[last_h], cross_recv.at[last_h], across_other)
     cross_lent = remote(lent_buf, q_out.at[last_h, partner_lent], lent_sem.at[2], lent_sem.at[3], across)
     my_early = pl.ds(pl.multiple_of(member * n_rows, n_rows), early)
-    early_far = remote(late_out.at[0, pl.ds(0, early)], q_out.at[1, my_early], early_sem.at[0], early_sem.at[1], across)
+    early_far = remote(late_out.at[last_h - 1, pl.ds(0, early)], q_out.at[last_h, my_early], early_sem.at[0], early_sem.at[1], across)
 
     for j in range(FIRST_HEAD):
         link[j].start()
@@ -308,16 +308,16 @@
 
     @pl.when(core == 1)
     def _():
+        cross[last_h].start()
+        far[FIRST_HEAD + 1].start()
         lend.wait_recv()
         cross_lent.start()
         early_far.start()
-        cross[last_h].start()
 
     @pl.when(core == 0)
     def _():
         cross_kept.start()
-        for copy in far[FIRST_HEAD:]:
-            copy.start()
+        far[FIRST_HEAD].start()
 
     for h in range(heads):
         part[FIRST_HEAD + h].wait_recv()
@@ -353,8 +353,6 @@
 
     @pl.when(core == 0)
     def _():
-        for copy in far[FIRST_HEAD + 1:]:
-            copy.wait()
         lend.wait_send()
         cross_kept.wait_send()
         cross[last_h].wait_recv()
@@ -362,91 +360,93 @@
     @pl.when(core == 1)
     def _():
         cross[last_h].wait_send()
+        far[FIRST_HEAD + 1].wait()
         early_far.wait()
         cross_lent.wait()
         cross_kept.wait_recv()
 
 
+def late_cuts(early, n_rows, core):
+    return [(0, 0, n_rows), (1, 0, n_rows)] if core == 0 else [(1, early, n_rows - early)]
+
+
 def finish_kernel(q_ref, k_ref, v_ref, q_out, k_out, v_out, sems, *, early):
     member = lax.axis_index("tp")
-    chip, core = member // 2, member % 2
+    core = member % 2
     n_rows = q_ref.shape[1] // 4
-    here, there = [], []
+    late_base = ((member + 2) % 4) * n_rows
+    always, one_only = [], []
+
+    def copy_of(ref, out, h, where):
+        return pltpu.make_async_copy(ref.at[h, where], out.at[h, where], sems.at[len(always) + len(one_only)])
+
     for ref, out in ((q_ref, q_out), (k_ref, k_out), (v_ref, v_out)):
         for h in range(ref.shape[0]):
             for cut in range(4):
-                where = pl.ds(pl.multiple_of(((3 - 2 * chip + cut + 1) % 4) * n_rows, n_rows), n_rows)
-                copy = pltpu.make_async_copy(ref.at[h, where], out.at[h, where], sems.at[len(here) + len(there)])
-                (there if cut == 3 and ref is q_ref and h else here).append(copy)
-
-    for copy in here:
+                where = pl.ds(pl.multiple_of(((member + 3 + cut) % 4) * n_rows, n_rows), n_rows)
+                if cut < 3 or ref is not q_ref or h == 0:
+                    always.append(copy_of(ref, out, h, where))
+                elif h == 1:
+                    one_only.append(copy_of(ref, out, h, where))
+                else:
+                    one_only.append(copy_of(ref, out, h, pl.ds(pl.multiple_of(late_base, n_rows), early)))
+
+    for copy in always:
         copy.start()
 
-    early_rows = pl.ds(pl.multiple_of((3 - 2 * chip) * n_rows, n_rows), early)
-    early_copy = pltpu.make_async_copy(q_ref.at[1, early_rows], q_out.at[1, early_rows], sems.at[len(here) + len(there)])
-
     @pl.when(core == 1)
     def _():
-        early_copy.start()
-
-    @pl.when(core == 0)
-    def _():
-        for copy in there:
+        for copy in one_only:
             copy.start()
 
-    for copy in here:
+    for copy in always:
         copy.wait()
 
     @pl.when(core == 1)
     def _():
-        early_copy.wait()
-
-    @pl.when(core == 0)
-    def _():
-        for copy in there:
+        for copy in one_only:
             copy.wait()
-
-
-def late_cut(early, n_rows, i):
-    return pl.ds(early, n_rows - early) if i == 0 else pl.ds(0, n_rows)
 
 
 def late_kernel(after_ref, late_out, late_in, send_sem, recv_sem, *, early):
     group, member = lax.axis_index("dp"), lax.axis_index("tp")
-
-    @pl.when(member % 2 == 1)
-    def _():
-        across = (group, (member + 2) % 4)
-        barrier = pltpu.get_barrier_semaphore()
-        pl.semaphore_signal(barrier, inc=1, device_id=across, device_id_type=MESH)
-        pl.semaphore_wait(barrier, 1)
-        copies = [
-            pltpu.make_async_remote_copy(src_ref=late_out.at[i, cut], dst_ref=late_in.at[i, cut], send_sem=send_sem.at[i],
-                                         recv_sem=recv_sem.at[i], device_id=across, device_id_type=MESH)
-            for i, cut in enumerate(late_cut(early, late_out.shape[1], i) for i in range(late_out.shape[0]))
-        ]
+    across = (group, (member + 2) % 4)
+    barrier = pltpu.get_barrier_semaphore()
+    pl.semaphore_signal(barrier, inc=1, device_id=across, device_id_type=MESH)
+    pl.semaphore_wait(barrier, 1)
+
+    def exchange(core):
+        copies = []
+        for i, start, size in late_cuts(early, late_out.shape[1], core):
+            cut = pl.ds(start, size)
+            copies.append(pltpu.make_async_remote_copy(src_ref=late_out.at[i, cut], dst_ref=late_in.at[i, cut], send_sem=send_sem.at[i],
+                                                       recv_sem=recv_sem.at[i], device_id=across, device_id_type=MESH))
         for copy in copies:
             copy.start()
         for copy in copies:
             copy.wait()
 
+    for core in range(2):
+        pl.when(member % 2 == core)(functools.partial(exchange, core))
+
 
 def patch_kernel(before_ref, late_ref, q_out, sems, *, early):
     member = lax.axis_index("tp")
     n_rows = late_ref.shape[1]
-
-    @pl.when(member % 2 == 1)
-    def _():
-        base = ((member + 2) % 4) * n_rows
+    base = ((member + 2) % 4) * n_rows
+
+    def put(core):
         copies = []
-        for i in range(late_ref.shape[0]):
-            cut = late_cut(early, n_rows, i)
-            where = pl.ds(pl.multiple_of(base + cut.start, early), cut.size)
-            copies.append(pltpu.make_async_copy(late_ref.at[i, cut], q_out.at[1 + i, where], sems.at[i]))
+        for i, start, size in late_cuts(early, n_rows, core):
+            where = pl.ds(pl.multiple_of(base + start, 64), size)
+            copies.append(pltpu.make_async_copy(late_ref.at[i, pl.ds(start, size)], q_out.at[1 + i, where], sems.at[i]))
         for copy in copies:
             copy.start()
         for copy in copies:
             copy.wait()
+
+    for core in range(2):
+        pl.when(member % 2 == core)(functools.partial(put, core))
 
 
 def solution(mesh):
@@ -459,7 +459,7 @@
         all_rows = members * n_rows
         dma = pltpu.SemaphoreType.DMA
         norm_tile = n_rows // 4
-        shift, lent, early = 56, 128, 128
+        shift, lent, early = 56, 640, 448
         vmem = pl.BlockSpec(memory_space=pltpu.VMEM)
         results = tuple(jax.ShapeDtypeStruct((n, all_rows, width), jnp.bfloat16) for n in (heads, 1, 1))
         hbm = pl.BlockSpec(memory_space=pltpu.HBM)
@@ -492,7 +492,7 @@
             out_shape=results,
             in_specs=[vmem] * 3,
             out_specs=(hbm,) * 3,
-            scratch_shapes=[dma((4 * (heads + 2) + 1,))],
+            scratch_shapes=[dma((4 * (heads + 2),))],
             compiler_params=pltpu.CompilerParams(vmem_limit_bytes=16 * 1024 * 1024),
             name="finish",
         )(q, k, v)

time: 66.1 us -> 67.3 us (1.018)
  Pallas kernels: 65.4 us -> 66.4 us
    pallas_call x1, Pallas kernels: 54.4 us -> 58.3 us  [local_step(): pl.pallas_call(functools.partial(qkv_kernel, norm_tile=norm_tile, dot_til...]
    pallas_call x1, Pallas kernels: 7.78 us -> 4.92 us  [local_step(): pl.pallas_call(functools.partial(late_kernel, early=early), out_shape=lat...]
where the time goes in v16:
time: 67.3 us; the launch traced here: 67.1 us
  Pallas kernels  66.4 us (99%)
    pallas_call x1, Pallas kernels, local_step(): pl.pallas_call(functools.partial(qkv_kernel, norm_tile=norm_tile, dot_til...  58.3 us
    pallas_call x1, Pallas kernels, local_step(): pl.pallas_call(functools.partial(late_kernel, early=early), out_shape=lat...  4.92 us
    pallas_call x1, Pallas kernels, local_step(): pl.pallas_call(functools.partial(finish_kernel, early=early), out_shape=r...  2.45 us

profile of v16, /device:TPU:1, one launch (start us, length us, event | category | flops | bytes accessed | tf_op | source)
XLA Modules:
  0.0 67.1 jit_solution(15346114168184289541)
XLA Ops:
  0.6 58.3 %qkv.1 = (bf16[3,4096,128]{2,1,0:T(8,128)(2,1)S(1)}, bf16[1,4096,128]{2,1,0:T(8,128)(2,1)S(1)}, bf16[1,4096,128]{2,1,0:T(8,128)(2,1)S(1)}, bf16[2,1024,128]{2,1,0:T(8,128)(2,1)S(1)}) custom-call(bf16[1024,1536]{1,0:T(8,128)(2,1)} %x_hbm.1, f32[1536]{0:T(1024)} %gain_hbm.1, bf16[3,1536,128]{2,1,0:T(8,128)(2,1)} %bitcast.7, bf16[64,1536]{1,0:T(8,128)(2,1)} %bitcast.10, ...), custom_call_target="tpu_custom_call" | custom-call | flops 6442450944 | bytes 16777216 | tf_op jit(solution)/shard_map/qkv/pallas_call | solution.py:467
  59.0 2.4 %finish.1 = (bf16[3,4096,128]{2,1,0:T(8,128)(2,1)}, bf16[1,4096,128]{2,1,0:T(8,128)(2,1)}, bf16[1,4096,128]{2,1,0:T(8,128)(2,1)}) custom-call(bf16[3,4096,128]{2,1,0:T(8,128)(2,1)S(1)} %get-tuple-element.10.q_ref, bf16[1,4096,128]{2,1,0:T(8,128)(2,1)S(1)} %get-tuple-element.11.k_ref, bf16[1,4096,128]{2,1,0:T(8,128)(2,1)S(1)} %get-tuple-element.12.v_ref), custom_call_target="tpu_custom_call" | custom-call | tf_op jit(solution)/shard_map/finish/pallas_call | solution.py:490
  61.4 4.9 %late.1.late_ref = bf16[2,1024,128]{2,1,0:T(8,128)(2,1)S(1)} custom-call(bf16[3,4096,128]{2,1,0:T(8,128)(2,1)} %get-tuple-element.13.after_ref.before_ref, bf16[2,1024,128]{2,1,0:T(8,128)(2,1)S(1)} %get-tuple-element.14.late_out), custom_call_target="tpu_custom_call" | custom-call | tf_op jit(solution)/shard_map/late/pallas_call | solution.py:499
  66.4 0.7 %patch.1 = bf16[3,4096,128]{2,1,0:T(8,128)(2,1)} custom-call(bf16[3,4096,128]{2,1,0:T(8,128)(2,1)} %get-tuple-element.13.after_ref.before_ref, bf16[2,1024,128]{2,1,0:T(8,128)(2,1)S(1)} %late.1.late_ref), custom_call_target="tpu_custom_call", output_to_operand_aliasing={{}: (0, {})} | custom-call | tf_op jit(solution)/shard_map/patch/pallas_call | solution.py:508

commit v17 on v15

--- a/solution.py
+++ b/solution.py
@@ -126,7 +126,7 @@
     cross_kept = remote(q_stage.at[2, last_h, kept_rows], q_out.at[last_h, my_kept], cross_send.at[last_h], cross_recv.at[last_h], across_other)
     cross_lent = remote(lent_buf, q_out.at[last_h, partner_lent], lent_sem.at[2], lent_sem.at[3], across)
     my_early = pl.ds(pl.multiple_of(member * n_rows, n_rows), early)
-    early_far = remote(late_out.at[0, pl.ds(0, early)], q_out.at[1, my_early], early_sem.at[0], early_sem.at[1], across)
+    early_far = remote(late_out.at[:, pl.ds(0, early)], q_out.at[pl.ds(1, heads - 1), my_early], early_sem.at[0], early_sem.at[1], across)
 
     for j in range(FIRST_HEAD):
         link[j].start()
@@ -369,46 +369,28 @@
 
 def finish_kernel(q_ref, k_ref, v_ref, q_out, k_out, v_out, sems, *, early):
     member = lax.axis_index("tp")
-    chip, core = member // 2, member % 2
-    n_rows = q_ref.shape[1] // 4
-    here, there = [], []
-    for ref, out in ((q_ref, q_out), (k_ref, k_out), (v_ref, v_out)):
-        for h in range(ref.shape[0]):
-            for cut in range(4):
-                where = pl.ds(pl.multiple_of(((3 - 2 * chip + cut + 1) % 4) * n_rows, n_rows), n_rows)
-                copy = pltpu.make_async_copy(ref.at[h, where], out.at[h, where], sems.at[len(here) + len(there)])
-                (there if cut == 3 and ref is q_ref and h else here).append(copy)
-
-    for copy in here:
+    core = member % 2
+    heads, n_rows = q_ref.shape[0], q_ref.shape[1] // 4
+    late_heads = pl.ds(1, heads - 1)
+
+    def copy_of(i, ref, out, *where):
+        return pltpu.make_async_copy(ref.at[where], out.at[where], sems.at[i])
+
+    def rows(ahead, size):
+        return pl.ds(pl.multiple_of(((member + ahead) % 4) * n_rows, n_rows), size)
+
+    always = [copy_of(i, q_ref, q_out, late_heads, rows(ahead, n_rows)) for i, ahead in enumerate((0, 1, 3))]
+    always += [copy_of(3, q_ref, q_out, 0), copy_of(4, k_ref, k_out, 0), copy_of(5, v_ref, v_out, 0)]
+    whole = copy_of(6, q_ref, q_out, late_heads, rows(2, n_rows))
+    begun = copy_of(6, q_ref, q_out, late_heads, rows(2, early))
+    for copy in always:
         copy.start()
-
-    early_rows = pl.ds(pl.multiple_of((3 - 2 * chip) * n_rows, n_rows), early)
-    early_copy = pltpu.make_async_copy(q_ref.at[1, early_rows], q_out.at[1, early_rows], sems.at[len(here) + len(there)])
-
-    @pl.when(core == 1)
-    def _():
-        early_copy.start()
-
-    @pl.when(core == 0)
-    def _():
-        for copy in there:
-            copy.start()
-
-    for copy in here:
+    pl.when(core == 0)(whole.start)
+    pl.when(core == 1)(begun.start)
+    for copy in always:
         copy.wait()
-
-    @pl.when(core == 1)
-    def _():
-        early_copy.wait()
-
-    @pl.when(core == 0)
-    def _():
-        for copy in there:
-            copy.wait()
-
-
-def late_cut(early, n_rows, i):
-    return pl.ds(early, n_rows - early) if i == 0 else pl.ds(0, n_rows)
+    pl.when(core == 0)(whole.wait)
+    pl.when(core == 1)(begun.wait)
 
 
 def late_kernel(after_ref, late_out, late_in, send_sem, recv_sem, *, early):
@@ -420,33 +402,24 @@
         barrier = pltpu.get_barrier_semaphore()
         pl.semaphore_signal(barrier, inc=1, device_id=across, device_id_type=MESH)
         pl.semaphore_wait(barrier, 1)
-        copies = [
-            pltpu.make_async_remote_copy(src_ref=late_out.at[i, cut], dst_ref=late_in.at[i, cut], send_sem=send_sem.at[i],
-                                         recv_sem=recv_sem.at[i], device_id=across, device_id_type=MESH)
-            for i, cut in enumerate(late_cut(early, late_out.shape[1], i) for i in range(late_out.shape[0]))
-        ]
-        for copy in copies:
-            copy.start()
-        for copy in copies:
-            copy.wait()
-
-
-def patch_kernel(before_ref, late_ref, q_out, sems, *, early):
+        rest = pl.ds(early, late_out.shape[1] - early)
+        copy = pltpu.make_async_remote_copy(src_ref=late_out.at[:, rest], dst_ref=late_in.at[:, rest], send_sem=send_sem, recv_sem=recv_sem,
+                                            device_id=across, device_id_type=MESH)
+        copy.start()
+        copy.wait()
+
+
+def patch_kernel(before_ref, late_ref, q_out, sem, *, early):
     member = lax.axis_index("tp")
-    n_rows = late_ref.shape[1]
+    late_heads, n_rows, _ = late_ref.shape
 
     @pl.when(member % 2 == 1)
     def _():
-        base = ((member + 2) % 4) * n_rows
-        copies = []
-        for i in range(late_ref.shape[0]):
-            cut = late_cut(early, n_rows, i)
-            where = pl.ds(pl.multiple_of(base + cut.start, early), cut.size)
-            copies.append(pltpu.make_async_copy(late_ref.at[i, cut], q_out.at[1 + i, where], sems.at[i]))
-        for copy in copies:
-            copy.start()
-        for copy in copies:
-            copy.wait()
+        size = n_rows - early
+        where = pl.ds(pl.multiple_of(((member + 2) % 4) * n_rows + early, early), size)
+        copy = pltpu.make_async_copy(late_ref.at[:, pl.ds(early, size)], q_out.at[pl.ds(1, late_heads), where], sem)
+        copy.start()
+        copy.wait()
 
 
 def solution(mesh):
@@ -459,7 +432,7 @@
         all_rows = members * n_rows
         dma = pltpu.SemaphoreType.DMA
         norm_tile = n_rows // 4
-        shift, lent, early = 56, 128, 128
+        shift, lent, early = 56, 128, 64
         vmem = pl.BlockSpec(memory_space=pltpu.VMEM)
         results = tuple(jax.ShapeDtypeStruct((n, all_rows, width), jnp.bfloat16) for n in (heads, 1, 1))
         hbm = pl.BlockSpec(memory_space=pltpu.HBM)
@@ -492,7 +465,7 @@
             out_shape=results,
             in_specs=[vmem] * 3,
             out_specs=(hbm,) * 3,
-            scratch_shapes=[dma((4 * (heads + 2) + 1,))],
+            scratch_shapes=[dma((7,))],
             compiler_params=pltpu.CompilerParams(vmem_limit_bytes=16 * 1024 * 1024),
             name="finish",
         )(q, k, v)
@@ -501,7 +474,7 @@
             out_shape=late_shape,
             in_specs=[hbm, vmem],
             out_specs=vmem,
-            scratch_shapes=[dma((heads - 1,)), dma((heads - 1,))],
+            scratch_shapes=[dma(()), dma(())],
             compiler_params=pltpu.CompilerParams(collective_id=1, has_side_effects=True, vmem_limit_bytes=16 * 1024 * 1024),
             name="late",
         )(pltpu.with_memory_space_constraint(q, pltpu.HBM), late)
@@ -510,7 +483,7 @@
             out_shape=results[0],
             in_specs=[hbm, vmem],
             out_specs=hbm,
-            scratch_shapes=[dma((heads - 1,))],
+            scratch_shapes=[dma(())],
             input_output_aliases={0: 0},
             compiler_params=pltpu.CompilerParams(vmem_limit_bytes=16 * 1024 * 1024),
             name="patch",

time: 66.1 us -> 66.1 us (level)
  no operation moved by 1% of the time
where the time goes in v17:
time: 66.1 us; the launch traced here: 66 us
  Pallas kernels  65.3 us (99%)
    pallas_call x1, Pallas kernels, local_step(): pl.pallas_call(functools.partial(qkv_kernel, norm_tile=norm_tile, dot_til...  54.4 us
    pallas_call x1, Pallas kernels, local_step(): pl.pallas_call(functools.partial(late_kernel, early=early), out_shape=lat...  7.87 us
    pallas_call x1, Pallas kernels, local_step(): pl.pallas_call(functools.partial(finish_kernel, early=early), out_shape=r...  2.26 us

profile of v17, /device:TPU:1, one launch (start us, length us, event | category | flops | bytes accessed | tf_op | source)
XLA Modules:
  0.0 66.0 jit_solution(10795229559213604412)
XLA Ops:
  0.6 54.4 %qkv.1 = (bf16[3,4096,128]{2,1,0:T(8,128)(2,1)S(1)}, bf16[1,4096,128]{2,1,0:T(8,128)(2,1)S(1)}, bf16[1,4096,128]{2,1,0:T(8,128)(2,1)S(1)}, bf16[2,1024,128]{2,1,0:T(8,128)(2,1)S(1)}) custom-call(bf16[1024,1536]{1,0:T(8,128)(2,1)} %x_hbm.1, f32[1536]{0:T(1024)} %gain_hbm.1, bf16[3,1536,128]{2,1,0:T(8,128)(2,1)} %bitcast.7, bf16[64,1536]{1,0:T(8,128)(2,1)} %bitcast.10, ...), custom_call_target="tpu_custom_call" | custom-call | flops 6442450944 | bytes 16777216 | tf_op jit(solution)/shard_map/qkv/pallas_call | solution.py:440
  55.0 2.3 %finish.1 = (bf16[3,4096,128]{2,1,0:T(8,128)(2,1)}, bf16[1,4096,128]{2,1,0:T(8,128)(2,1)}, bf16[1,4096,128]{2,1,0:T(8,128)(2,1)}) custom-call(bf16[3,4096,128]{2,1,0:T(8,128)(2,1)S(1)} %get-tuple-element.10.q_ref, bf16[1,4096,128]{2,1,0:T(8,128)(2,1)S(1)} %get-tuple-element.11.k_ref, bf16[1,4096,128]{2,1,0:T(8,128)(2,1)S(1)} %get-tuple-element.12.v_ref), custom_call_target="tpu_custom_call" | custom-call | tf_op jit(solution)/shard_map/finish/pallas_call | solution.py:463
  57.3 7.9 %late.1.late_ref = bf16[2,1024,128]{2,1,0:T(8,128)(2,1)S(1)} custom-call(bf16[3,4096,128]{2,1,0:T(8,128)(2,1)} %get-tuple-element.13.after_ref.before_ref, bf16[2,1024,128]{2,1,0:T(8,128)(2,1)S(1)} %get-tuple-element.14.late_out), custom_call_target="tpu_custom_call" | custom-call | tf_op jit(solution)/shard_map/late/pallas_call | solution.py:472
  65.2 0.8 %patch.1 = bf16[3,4096,128]{2,1,0:T(8,128)(2,1)} custom-call(bf16[3,4096,128]{2,1,0:T(8,128)(2,1)} %get-tuple-element.13.after_ref.before_ref, bf16[2,1024,128]{2,1,0:T(8,128)(2,1)S(1)} %late.1.late_ref), custom_call_target="tpu_custom_call", output_to_operand_aliasing={{}: (0, {})} | custom-call | tf_op jit(solution)/shard_map/patch/pallas_call | solution.py:481

commit v18 on v17

--- a/solution.py
+++ b/solution.py
@@ -30,7 +30,7 @@
     pieces = FIRST_HEAD + heads
 
     group, member = lax.axis_index("dp"), lax.axis_index("tp")
-    chip, core = member // 2, member % 2
+    chip, core = lax.div(member, 2), lax.rem(member, 2)
     partner = (group, chip * 2 + (1 - core))
     across = (group, (1 - chip) * 2 + core)
     across_other = (group, (1 - chip) * 2 + (1 - core))
@@ -125,8 +125,10 @@
     lend = remote(q_stage.at[2, last_h, lent_rows], lent_buf, lent_sem.at[0], lent_sem.at[1], partner)
     cross_kept = remote(q_stage.at[2, last_h, kept_rows], q_out.at[last_h, my_kept], cross_send.at[last_h], cross_recv.at[last_h], across_other)
     cross_lent = remote(lent_buf, q_out.at[last_h, partner_lent], lent_sem.at[2], lent_sem.at[3], across)
-    my_early = pl.ds(pl.multiple_of(member * n_rows, n_rows), early)
-    early_far = remote(late_out.at[:, pl.ds(0, early)], q_out.at[pl.ds(1, heads - 1), my_early], early_sem.at[0], early_sem.at[1], across)
+    early_far = []
+    for rows in early:
+        my_early = pl.ds(pl.multiple_of(member * n_rows, n_rows), rows)
+        early_far.append(remote(late_out.at[:, pl.ds(0, rows)], q_out.at[pl.ds(1, heads - 1), my_early], early_sem.at[0], early_sem.at[1], across))
 
     for j in range(FIRST_HEAD):
         link[j].start()
@@ -310,7 +312,8 @@
     def _():
         lend.wait_recv()
         cross_lent.start()
-        early_far.start()
+        for c in range(2):
+            when(chip == c, early_far[c].start)
         cross[last_h].start()
 
     @pl.when(core == 0)
@@ -362,7 +365,9 @@
     @pl.when(core == 1)
     def _():
         cross[last_h].wait_send()
-        early_far.wait()
+        for c in range(2):
+            when(chip == c, early_far[c].wait_send)
+            when(chip == c, early_far[1 - c].wait_recv)
         cross_lent.wait()
         cross_kept.wait_recv()
 
@@ -382,44 +387,54 @@
     always = [copy_of(i, q_ref, q_out, late_heads, rows(ahead, n_rows)) for i, ahead in enumerate((0, 1, 3))]
     always += [copy_of(3, q_ref, q_out, 0), copy_of(4, k_ref, k_out, 0), copy_of(5, v_ref, v_out, 0)]
     whole = copy_of(6, q_ref, q_out, late_heads, rows(2, n_rows))
-    begun = copy_of(6, q_ref, q_out, late_heads, rows(2, early))
+    begun = [copy_of(6, q_ref, q_out, late_heads, rows(2, early[1 - chip])) for chip in range(2)]
     for copy in always:
         copy.start()
     pl.when(core == 0)(whole.start)
-    pl.when(core == 1)(begun.start)
+    for chip in range(2):
+        pl.when(member == 2 * chip + 1)(begun[chip].start)
     for copy in always:
         copy.wait()
     pl.when(core == 0)(whole.wait)
-    pl.when(core == 1)(begun.wait)
+    for chip in range(2):
+        pl.when(member == 2 * chip + 1)(begun[chip].wait)
 
 
 def late_kernel(after_ref, late_out, late_in, send_sem, recv_sem, *, early):
     group, member = lax.axis_index("dp"), lax.axis_index("tp")
 
-    @pl.when(member % 2 == 1)
-    def _():
-        across = (group, (member + 2) % 4)
+    def exchange(chip):
+        across = (group, 2 * (1 - chip) + 1)
         barrier = pltpu.get_barrier_semaphore()
         pl.semaphore_signal(barrier, inc=1, device_id=across, device_id_type=MESH)
         pl.semaphore_wait(barrier, 1)
-        rest = pl.ds(early, late_out.shape[1] - early)
-        copy = pltpu.make_async_remote_copy(src_ref=late_out.at[:, rest], dst_ref=late_in.at[:, rest], send_sem=send_sem, recv_sem=recv_sem,
-                                            device_id=across, device_id_type=MESH)
-        copy.start()
-        copy.wait()
+        copies = []
+        for rows in early:
+            rest = pl.ds(rows, late_out.shape[1] - rows)
+            copies.append(pltpu.make_async_remote_copy(src_ref=late_out.at[:, rest], dst_ref=late_in.at[:, rest], send_sem=send_sem,
+                                                       recv_sem=recv_sem, device_id=across, device_id_type=MESH))
+        copies[chip].start()
+        copies[chip].wait_send()
+        copies[1 - chip].wait_recv()
+
+    for chip in range(2):
+        pl.when(member == 2 * chip + 1)(functools.partial(exchange, chip))
 
 
 def patch_kernel(before_ref, late_ref, q_out, sem, *, early):
     member = lax.axis_index("tp")
     late_heads, n_rows, _ = late_ref.shape
 
-    @pl.when(member % 2 == 1)
-    def _():
-        size = n_rows - early
-        where = pl.ds(pl.multiple_of(((member + 2) % 4) * n_rows + early, early), size)
-        copy = pltpu.make_async_copy(late_ref.at[:, pl.ds(early, size)], q_out.at[pl.ds(1, late_heads), where], sem)
+    def put(chip):
+        start = early[1 - chip]
+        base = (2 * (1 - chip) + 1) * n_rows
+        copy = pltpu.make_async_copy(late_ref.at[:, pl.ds(start, n_rows - start)],
+                                     q_out.at[pl.ds(1, late_heads), pl.ds(base + start, n_rows - start)], sem)
         copy.start()
         copy.wait()
+
+    for chip in range(2):
+        pl.when(member == 2 * chip + 1)(functools.partial(put, chip))
 
 
 def solution(mesh):
@@ -432,7 +447,7 @@
         all_rows = members * n_rows
         dma = pltpu.SemaphoreType.DMA
         norm_tile = n_rows // 4
-        shift, lent, early = 56, 128, 64
+        shift, lent, early = 56, 128, (64, 128)
         vmem = pl.BlockSpec(memory_space=pltpu.VMEM)
         results = tuple(jax.ShapeDtypeStruct((n, all_rows, width), jnp.bfloat16) for n in (heads, 1, 1))
         hbm = pl.BlockSpec(memory_space=pltpu.HBM)

time: 66.1 us -> 66.1 us (level)
  no operation moved by 1% of the time
where the time goes in v18:
time: 66.1 us; the launch traced here: 66 us
  Pallas kernels  65.3 us (99%)
    pallas_call x1, Pallas kernels, local_step(): pl.pallas_call(functools.partial(qkv_kernel, norm_tile=norm_tile, dot_til...  54.4 us
    pallas_call x1, Pallas kernels, local_step(): pl.pallas_call(functools.partial(late_kernel, early=early), out_shape=lat...  7.87 us
    pallas_call x1, Pallas kernels, local_step(): pl.pallas_call(functools.partial(finish_kernel, early=early), out_shape=r...  2.26 us

profile of v18, /device:TPU:1, one launch (start us, length us, event | category | flops | bytes accessed | tf_op | source)
XLA Modules:
  0.0 66.0 jit_solution(15266938100964816846)
XLA Ops:
  0.6 54.4 %qkv.1 = (bf16[3,4096,128]{2,1,0:T(8,128)(2,1)S(1)}, bf16[1,4096,128]{2,1,0:T(8,128)(2,1)S(1)}, bf16[1,4096,128]{2,1,0:T(8,128)(2,1)S(1)}, bf16[2,1024,128]{2,1,0:T(8,128)(2,1)S(1)}) custom-call(bf16[1024,1536]{1,0:T(8,128)(2,1)} %x_hbm.1, f32[1536]{0:T(1024)} %gain_hbm.1, bf16[3,1536,128]{2,1,0:T(8,128)(2,1)} %bitcast.7, bf16[64,1536]{1,0:T(8,128)(2,1)} %bitcast.10, ...), custom_call_target="tpu_custom_call" | custom-call | flops 6442450944 | bytes 16777216 | tf_op jit(solution)/shard_map/qkv/pallas_call | solution.py:455
  55.0 2.3 %finish.1 = (bf16[3,4096,128]{2,1,0:T(8,128)(2,1)}, bf16[1,4096,128]{2,1,0:T(8,128)(2,1)}, bf16[1,4096,128]{2,1,0:T(8,128)(2,1)}) custom-call(bf16[3,4096,128]{2,1,0:T(8,128)(2,1)S(1)} %get-tuple-element.10.q_ref, bf16[1,4096,128]{2,1,0:T(8,128)(2,1)S(1)} %get-tuple-element.11.k_ref, bf16[1,4096,128]{2,1,0:T(8,128)(2,1)S(1)} %get-tuple-element.12.v_ref), custom_call_target="tpu_custom_call" | custom-call | tf_op jit(solution)/shard_map/finish/pallas_call | solution.py:478
  57.3 7.9 %late.1.late_ref = bf16[2,1024,128]{2,1,0:T(8,128)(2,1)S(1)} custom-call(bf16[3,4096,128]{2,1,0:T(8,128)(2,1)} %get-tuple-element.13.after_ref.before_ref, bf16[2,1024,128]{2,1,0:T(8,128)(2,1)S(1)} %get-tuple-element.14.late_out), custom_call_target="tpu_custom_call" | custom-call | tf_op jit(solution)/shard_map/late/pallas_call | solution.py:487
  65.2 0.8 %patch.1 = bf16[3,4096,128]{2,1,0:T(8,128)(2,1)} custom-call(bf16[3,4096,128]{2,1,0:T(8,128)(2,1)} %get-tuple-element.13.after_ref.before_ref, bf16[2,1024,128]{2,1,0:T(8,128)(2,1)S(1)} %late.1.late_ref), custom_call_target="tpu_custom_call", output_to_operand_aliasing={{}: (0, {})} | custom-call | tf_op jit(solution)/shard_map/patch/pallas_call | solution.py:496

commit v19 on v18

--- a/solution.py
+++ b/solution.py
@@ -447,7 +447,7 @@
         all_rows = members * n_rows
         dma = pltpu.SemaphoreType.DMA
         norm_tile = n_rows // 4
-        shift, lent, early = 56, 128, (64, 128)
+        shift, lent, early = 56, 32, (112, 176)
         vmem = pl.BlockSpec(memory_space=pltpu.VMEM)
         results = tuple(jax.ShapeDtypeStruct((n, all_rows, width), jnp.bfloat16) for n in (heads, 1, 1))
         hbm = pl.BlockSpec(memory_space=pltpu.HBM)

time: 66.1 us -> 66.1 us (level)
  no operation moved by 1% of the time
where the time goes in v19:
time: 66.1 us; the launch traced here: 66 us
  Pallas kernels  65.3 us (99%)
    pallas_call x1, Pallas kernels, local_step(): pl.pallas_call(functools.partial(qkv_kernel, norm_tile=norm_tile, dot_til...  54.4 us
    pallas_call x1, Pallas kernels, local_step(): pl.pallas_call(functools.partial(late_kernel, early=early), out_shape=lat...  7.86 us
    pallas_call x1, Pallas kernels, local_step(): pl.pallas_call(functools.partial(finish_kernel, early=early), out_shape=r...  2.27 us

profile of v19, /device:TPU:1, one launch (start us, length us, event | category | flops | bytes accessed | tf_op | source)
XLA Modules:
  0.0 66.0 jit_solution(14698040465818926156)
XLA Ops:
  0.6 54.4 %qkv.1 = (bf16[3,4096,128]{2,1,0:T(8,128)(2,1)S(1)}, bf16[1,4096,128]{2,1,0:T(8,128)(2,1)S(1)}, bf16[1,4096,128]{2,1,0:T(8,128)(2,1)S(1)}, bf16[2,1024,128]{2,1,0:T(8,128)(2,1)S(1)}) custom-call(bf16[1024,1536]{1,0:T(8,128)(2,1)} %x_hbm.1, f32[1536]{0:T(1024)} %gain_hbm.1, bf16[3,1536,128]{2,1,0:T(8,128)(2,1)} %bitcast.7, bf16[64,1536]{1,0:T(8,128)(2,1)} %bitcast.10, ...), custom_call_target="tpu_custom_call" | custom-call | flops 6442450944 | bytes 16777216 | tf_op jit(solution)/shard_map/qkv/pallas_call | solution.py:455
  55.0 2.3 %finish.1 = (bf16[3,4096,128]{2,1,0:T(8,128)(2,1)}, bf16[1,4096,128]{2,1,0:T(8,128)(2,1)}, bf16[1,4096,128]{2,1,0:T(8,128)(2,1)}) custom-call(bf16[3,4096,128]{2,1,0:T(8,128)(2,1)S(1)} %get-tuple-element.10.q_ref, bf16[1,4096,128]{2,1,0:T(8,128)(2,1)S(1)} %get-tuple-element.11.k_ref, bf16[1,4096,128]{2,1,0:T(8,128)(2,1)S(1)} %get-tuple-element.12.v_ref), custom_call_target="tpu_custom_call" | custom-call | tf_op jit(solution)/shard_map/finish/pallas_call | solution.py:478
  57.3 7.9 %late.1.late_ref = bf16[2,1024,128]{2,1,0:T(8,128)(2,1)S(1)} custom-call(bf16[3,4096,128]{2,1,0:T(8,128)(2,1)} %get-tuple-element.13.after_ref.before_ref, bf16[2,1024,128]{2,1,0:T(8,128)(2,1)S(1)} %get-tuple-element.14.late_out), custom_call_target="tpu_custom_call" | custom-call | tf_op jit(solution)/shard_map/late/pallas_call | solution.py:487
  65.2 0.8 %patch.1 = bf16[3,4096,128]{2,1,0:T(8,128)(2,1)} custom-call(bf16[3,4096,128]{2,1,0:T(8,128)(2,1)} %get-tuple-element.13.after_ref.before_ref, bf16[2,1024,128]{2,1,0:T(8,128)(2,1)S(1)} %late.1.late_ref), custom_call_target="tpu_custom_call", output_to_operand_aliasing={{}: (0, {})} | custom-call | tf_op jit(solution)/shard_map/patch/pallas_call | solution.py:496

commit v20 on v19

--- a/solution.py
+++ b/solution.py
@@ -447,7 +447,7 @@
         all_rows = members * n_rows
         dma = pltpu.SemaphoreType.DMA
         norm_tile = n_rows // 4
-        shift, lent, early = 56, 32, (112, 176)
+        shift, lent, early = 48, 32, (112, 176)
         vmem = pl.BlockSpec(memory_space=pltpu.VMEM)
         results = tuple(jax.ShapeDtypeStruct((n, all_rows, width), jnp.bfloat16) for n in (heads, 1, 1))
         hbm = pl.BlockSpec(memory_space=pltpu.HBM)

time: 66.1 us -> 66.1 us (level)
  no operation moved by 1% of the time
where the time goes in v20:
time: 66.1 us; the launch traced here: 66 us
  Pallas kernels  65.3 us (99%)
    pallas_call x1, Pallas kernels, local_step(): pl.pallas_call(functools.partial(qkv_kernel, norm_tile=norm_tile, dot_til...  54.4 us
    pallas_call x1, Pallas kernels, local_step(): pl.pallas_call(functools.partial(late_kernel, early=early), out_shape=lat...  7.91 us
    pallas_call x1, Pallas kernels, local_step(): pl.pallas_call(functools.partial(finish_kernel, early=early), out_shape=r...  2.27 us

profile of v20, /device:TPU:1, one launch (start us, length us, event | category | flops | bytes accessed | tf_op | source)
XLA Modules:
  0.0 66.0 jit_solution(1534318322384726749)
XLA Ops:
  0.6 54.4 %qkv.1 = (bf16[3,4096,128]{2,1,0:T(8,128)(2,1)S(1)}, bf16[1,4096,128]{2,1,0:T(8,128)(2,1)S(1)}, bf16[1,4096,128]{2,1,0:T(8,128)(2,1)S(1)}, bf16[2,1024,128]{2,1,0:T(8,128)(2,1)S(1)}) custom-call(bf16[1024,1536]{1,0:T(8,128)(2,1)} %x_hbm.1, f32[1536]{0:T(1024)} %gain_hbm.1, bf16[3,1536,128]{2,1,0:T(8,128)(2,1)} %bitcast.7, bf16[64,1536]{1,0:T(8,128)(2,1)} %bitcast.10, ...), custom_call_target="tpu_custom_call" | custom-call | flops 6442450944 | bytes 16777216 | tf_op jit(solution)/shard_map/qkv/pallas_call | solution.py:455
  55.0 2.3 %finish.1 = (bf16[3,4096,128]{2,1,0:T(8,128)(2,1)}, bf16[1,4096,128]{2,1,0:T(8,128)(2,1)}, bf16[1,4096,128]{2,1,0:T(8,128)(2,1)}) custom-call(bf16[3,4096,128]{2,1,0:T(8,128)(2,1)S(1)} %get-tuple-element.10.q_ref, bf16[1,4096,128]{2,1,0:T(8,128)(2,1)S(1)} %get-tuple-element.11.k_ref, bf16[1,4096,128]{2,1,0:T(8,128)(2,1)S(1)} %get-tuple-element.12.v_ref), custom_call_target="tpu_custom_call" | custom-call | tf_op jit(solution)/shard_map/finish/pallas_call | solution.py:478
  57.3 7.9 %late.1.late_ref = bf16[2,1024,128]{2,1,0:T(8,128)(2,1)S(1)} custom-call(bf16[3,4096,128]{2,1,0:T(8,128)(2,1)} %get-tuple-element.13.after_ref.before_ref, bf16[2,1024,128]{2,1,0:T(8,128)(2,1)S(1)} %get-tuple-element.14.late_out), custom_call_target="tpu_custom_call" | custom-call | tf_op jit(solution)/shard_map/late/pallas_call | solution.py:487
  65.2 0.8 %patch.1 = bf16[3,4096,128]{2,1,0:T(8,128)(2,1)} custom-call(bf16[3,4096,128]{2,1,0:T(8,128)(2,1)} %get-tuple-element.13.after_ref.before_ref, bf16[2,1024,128]{2,1,0:T(8,128)(2,1)S(1)} %late.1.late_ref), custom_call_target="tpu_custom_call", output_to_operand_aliasing={{}: (0, {})} | custom-call | tf_op jit(solution)/shard_map/patch/pallas_call | solution.py:496
